TPU v7x, 32 devices: a whole 2x2x4 slice. The times are simulated.
32 devices in a mesh: expert: 8 (over z, y), gate: 4 (over x, core).
Axes of the slice: x: 2, y: 2, z: 4, core: 2. Of those that a mesh axis runs over, the one named last changes fastest.
Arguments:
- samples: bfloat16 [6144, 4096], P('expert', 'gate'), may hold values from -4 to 4
- gate_weight: bfloat16 [4096, 32], P('gate'), may hold values from -1 to 1
- expert_ids: int32 [6144, 2], P('expert'), may hold values from 0 to 31, all different within a row; in each aligned block of 768 rows (0 to 767, 768 to 1535, ...) at most 96 rows name the same one
- pad_mask: int32 [6144], P('expert'), may hold values 0 or 1
- up_weight: bfloat16 [32, 4096, 1024], P(('expert', 'gate')), may hold values from -0.09375 to 0.09375
- down_weight: bfloat16 [32, 1024, 1024], P(('expert', 'gate')), may hold values from -0.1875 to 0.1875
Outputs:
- combined: bfloat16 [6144, 1024], P('expert', 'gate')
Inputs may be any that keep to these rules, and one draw needn't show every extreme that they name: `expert_ids`: each sample names two different experts; among the 768 samples of one index of expert no expert is named more than 96 times, a bound that some block reaches.
All inputs are finite; a program needn't handle non-finite values. No bound on the sum of `pad_mask` on one device may be relied on, other than what follows from the above.
Results may differ from a plain program's by a relative error of at most 0.0057.
Values may be sent and summed in bfloat16 or wider, within the bound.
No kernel may reach another device: no remote copies, remote signals or barrier semaphores. Data moves between devices by JAX's collectives and lax.ppermute only.
A program may use at most 128 MiB of HBM per device.

v0:
```python
import jax
import jax.numpy as jnp
from jax import lax
from jax.sharding import PartitionSpec as P


def joined(shard, axis, combine):
    everything = jax.tree.map(lambda part: lax.all_gather(part, axis), shard)
    leading = jax.tree.map(lambda part: part[0], everything)

    def step(k, so_far):
        return combine(so_far, jax.tree.map(lambda part: part[k], everything))

    return lax.fori_loop(1, lax.axis_size(axis), step, leading)


def combine_parts(first, second):
    row_top = jnp.maximum(first[0], second[0])
    left_scale = jnp.exp(first[0] - row_top)
    right_scale = jnp.exp(second[0] - row_top)
    row_total = first[1] * left_scale + second[1] * right_scale
    chosen = first[2] * left_scale[None, :] + second[2] * right_scale[None, :]
    return (row_top, row_total, chosen)


def per_device(samples, gate_weight, expert_ids, pad_mask, up_weight, down_weight):
    row_count = samples.shape[0]
    group_count = lax.axis_size("expert")
    gate_count = lax.axis_size("gate")
    expert_count = group_count * gate_count
    capacity = 4 * row_count // expert_count
    col_count = expert_count // gate_count
    gate_index = lax.axis_index("gate")
    logits_t = lax.psum_scatter(
        lax.dot_general(
            gate_weight, samples, (((0,), (1,)), ((), ())), preferred_element_type=jnp.float32
        ),
        "gate",
        scatter_dimension=0,
        tiled=True,
    )
    flat_ids = expert_ids.reshape(-1)
    onehot = (flat_ids[:, None] == jnp.arange(expert_count, dtype=jnp.int32)[None, :]).astype(
        jnp.int32
    )
    slot_rank = jnp.sum(onehot * (jnp.cumsum(onehot, axis=0) - 1), axis=1)
    position = flat_ids * capacity + slot_rank
    row_index = jnp.repeat(jnp.arange(row_count, dtype=jnp.int32), 2)
    owners = jnp.full((expert_count * capacity,), row_count, jnp.int32).at[position].set(row_index)
    whole_rows = lax.all_gather(samples, "gate", axis=1, tiled=True)
    padded = jnp.concatenate(
        [whole_rows, jnp.zeros((1, whole_rows.shape[1]), whole_rows.dtype)], axis=0
    )
    column_owners = lax.dynamic_index_in_dim(
        owners.reshape(group_count, gate_count, capacity), gate_index, 1, keepdims=False
    )
    outgoing = padded[column_owners]
    incoming = lax.all_to_all(outgoing, "expert", split_axis=0, concat_axis=0, tiled=True)
    slot_rows = incoming.reshape(group_count * capacity, whole_rows.shape[1])
    hidden = jnp.dot(slot_rows, up_weight[0], preferred_element_type=jnp.float32)
    active = jnp.maximum(hidden, 0.0).astype(jnp.bfloat16)
    expert_out = jnp.dot(active, down_weight[0], preferred_element_type=jnp.float32).astype(
        jnp.bfloat16
    )
    out_share = expert_out.shape[1] // gate_count
    outbound = expert_out.reshape(group_count, 1, 1, capacity, gate_count, out_share)
    returned = lax.all_to_all(
        lax.all_to_all(outbound, "expert", split_axis=0, concat_axis=1, tiled=True),
        "gate",
        split_axis=4,
        concat_axis=2,
        tiled=True,
    )
    returned = returned.reshape(expert_count * capacity, out_share)
    offset = expert_ids - gate_index * col_count
    inside = ((offset >= 0) & (offset < col_count)).T
    chosen = jnp.take_along_axis(logits_t, jnp.clip(offset, 0, col_count - 1).T, axis=0)
    local_top = jnp.max(logits_t, axis=0)
    local_total = jnp.sum(jnp.exp(logits_t - local_top[None, :]), axis=0)
    local_chosen = jnp.where(inside, jnp.exp(chosen - local_top[None, :]), 0.0)
    row_top, row_total, numerator = joined(
        (local_top, local_total, local_chosen), "gate", combine_parts
    )
    factor = expert_count * numerator / row_total[None, :] * pad_mask.astype(jnp.float32)[None, :]
    picked = returned[position].astype(jnp.float32).reshape(row_count, 2, out_share)
    mixed = factor[0][:, None] * picked[:, 0, :] + factor[1][:, None] * picked[:, 1, :]
    return mixed.astype(jnp.bfloat16)


def solution(mesh):
    placed = (
        P("expert", "gate"),
        P("gate", None),
        P("expert", None),
        P("expert"),
        P(("expert", "gate"), None, None),
        P(("expert", "gate"), None, None),
    )
    return jax.shard_map(
        per_device, mesh=mesh, in_specs=placed, out_specs=P("expert", "gate"), check_vma=False
    )
```

profile of v0, /device:TPU:0, one launch (start us, length us, event | category | flops | bytes accessed | tf_op | source)
XLA Modules:
  0.0 345.1 jit_solution(15891063067835120710)
XLA Ops:
  6.5 0.0 copy-start
  6.5 0.0 all-gather.8.cloned.1.call-start
  6.5 0.7 all-gather.8.cloned.1.call-update
  7.3 0.9 copy.19
  8.1 0.2 eq.29
  8.4 0.2 eq.25
  8.6 0.7 broadcast_multiply_fusion
  9.3 0.2 copy.18
  9.5 0.3 mul.137
  9.8 9.1 %reduce-window.6 = s32[32,12,128]{2,1,0:T(8,128)S(1)} reduce-window(s32[32,12,128]{2,1,0:T(8,128)S(1)} %fusion.14, s32[]{:T(128)} %constant.77.clone.1), window={size=1x1x128 pad=0_0x0_0x127_0}, to_apply=%region_5.6 | reduce-window | flops 6242304 | bytes 393220 | tf_op jit(solution)/shard_map/reduce-window
  18.8 0.1 slice.52
  19.0 0.2 copy.21
  19.2 0.1 copy.22
  19.3 0.2 reshape.149
  19.6 0.1 add_add_fusion
  19.7 0.1 fusion.16
  19.8 6.2 %scatter_custom_fusion = s32[3072]{0:T(1024)S(1)} fusion(s32[1536]{0:T(1024)S(1)} %fusion.17, s32[1536]{0:T(1024)S(1)} %reshape.149, s32[]{:T(128)} %constant.86.clone.1), kind=kCustom, calls=%fused_computation.44 | custom fusion | bytes 12292 | tf_op jit(solution)/shard_map/scatter | solution.py:49
  26.0 0.1 reshape.118
  26.1 0.1 reshape.125
  26.2 31.8 %all-gather.8.cloned.1.call-done = bf16[768,4096]{1,0:T(8,128)(2,1)} async-done(((bf16[768,1024]{1,0:T(8,128)(2,1)}), bf16[768,4096]{1,0:T(8,128)(2,1)}) %all-gather.8.cloned.1.call-update) | async-done | bytes 6291472 | tf_op jit(solution)/shard_map/all_gather | solution.py:50
  58.0 6.2 %concatenate.3 = bf16[769,4096]{1,0:T(8,128)(2,1)} pad(bf16[768,4096]{1,0:T(8,128)(2,1)} %all-gather.8.cloned.1.call-done, bf16[]{:T(256)} %constant.85.clone.1), padding=0_1x0_0 | pad | bytes 12591106 | tf_op jit(solution)/shard_map/concatenate | solution.py:51
  64.3 15.6 %gather_fusion = bf16[768,4096]{1,0:T(8,128)(2,1)} fusion(bf16[769,4096]{1,0:T(8,128)(2,1)} %concatenate.3, s32[1024]{0:T(1024)S(1)} %pad_clamp_fusion.1), kind=kCustom, calls=%fused_computation | custom fusion | bytes 12585984 | tf_op jit(solution)/shard_map/gather | solution.py:57
  79.8 144.1 %all_to_all.32 = bf16[8,96,4096]{2,1,0:T(8,128)(2,1)} all-to-all(bf16[8,96,4096]{2,1,0:T(8,128)(2,1)} %bitcast.93), channel_id=1, replica_groups=mesh['expert'=8,'gate'=4] {'expert'}, dimensions={0} | all-to-all | bytes 12582912 | tf_op jit(solution)/shard_map/all_to_all | solution.py:58
  223.9 0.0 copy-done
  224.0 14.6 %fusion.7 = bf16[768,1024]{1,0:T(8,128)(2,1)} fusion(bf16[1,1024,1024]{2,1,0:T(8,128)(2,1)S(1)} %copy-done, bf16[768,4096]{1,0:T(8,128)(2,1)} %bitcast.94, bf16[1,4096,1024]{2,1,0:T(8,128)(2,1)} %param.12), kind=kOutput, calls=%fused_computation.16 | convolution fusion | flops 8055422976 | bytes 18350080 | tf_op jit(solution)/shard_map/dot_general | solution.py:62
  238.6 0.0 copy-start.3
  238.6 3.9 %reshape.120 = bf16[8,1,1,96,4,256]{5,4,3,0,2,1:T(4,128)(2,1)} reshape(bf16[768,1024]{1,0:T(8,128)(2,1)} %fusion.7) | data formatting | bytes 3145728 | tf_op jit(solution)/shard_map/reshape | solution.py:66
  242.5 0.0 copy-start.2
  242.5 0.0 copy-start.4
  242.5 4.4 %all-to-all-start.1 = ((bf16[8,1,1,96,4,256]{5,4,3,2,1,0:T(4,128)(2,1)}), bf16[8,1,1,96,4,256]{5,4,3,2,1,0:T(4,128)(2,1)}, u32[]{:S(2)}, u32[]{:S(2)}) async-start(bf16[8,1,1,96,4,256]{5,4,3,2,1,0:T(4,128)(2,1)} %bitcast.95), calls=%async_computation.2 | async-start | bytes 3145728 | tf_op jit(solution)/shard_map/all_to_all | solution.py:68
  246.9 0.0 reduce-scatter.2.cloned.1.call-start
  247.0 0.0 copy-done.3
  247.0 2.6 fusion.23
  249.6 0.0 reduce-scatter.2.cloned.1.call-update
  249.6 0.0 copy-done.2
  249.7 0.0 copy-done.4
  249.7 20.5 %reduce-scatter.2.cloned.1.call-done = f32[8,768]{1,0:T(8,128)} async-done(((f32[32,768]{1,0:T(8,128)}), f32[8,768]{1,0:T(8,128)}) %reduce-scatter.2.cloned.1.call-update) | async-done | bytes 24592 | tf_op jit(solution)/shard_map/reduce_scatter | solution.py:34
  270.2 0.0 copy-start.1
  270.2 0.8 reduce_max.9
  271.0 0.8 exponential_reduce_fusion
  271.8 0.0 copy-done.1
  271.8 9.4 %gather_fusion.2 = f32[1536]{0:T(1024)S(1)} fusion(f32[8,768]{1,0:T(8,128)S(1)} %copy-done.1, s32[1536]{0:T(1024)S(1)} %reshape.139), kind=kCustom, calls=%fused_computation.2 | custom fusion | bytes 24576 | tf_op jit(solution)/shard_map/jit(take_along_axis)/gather | solution.py:77
  281.2 5.2 %all-gather.3 = f32[4,1,768]{2,1,0:T(1,128)S(1)} all-gather(f32[1,1,768]{2,1,0:T(1,128)S(1)} %reshape.168), channel_id=2, replica_groups=mesh['expert'=8,'gate'=4] {'gate'}, dimensions={0}, use_global_device_ids=true | all-gather | bytes 15360 | tf_op jit(solution)/shard_map/all_gather | solution.py:8
  286.4 5.2 %all-gather.4 = f32[4,1,768]{2,1,0:T(1,128)S(1)} all-gather(f32[1,1,768]{2,1,0:T(1,128)S(1)} %reshape.170), channel_id=3, replica_groups=mesh['expert'=8,'gate'=4] {'gate'}, dimensions={0}, use_global_device_ids=true | all-gather | bytes 15360 | tf_op jit(solution)/shard_map/all_gather | solution.py:8
  291.6 5.2 %all-gather.5 = f32[4,2,768]{2,1,0:T(2,128)S(1)} all-gather(f32[1,2,768]{2,1,0:T(2,128)S(1)} %fusion.19), channel_id=4, replica_groups=mesh['expert'=8,'gate'=4] {'gate'}, dimensions={0}, use_global_device_ids=true | all-gather | bytes 30720 | tf_op jit(solution)/shard_map/all_gather | solution.py:8
  296.8 0.0 all-to-all-done.1
  296.8 2.8 copy.24
  299.7 4.3 %all-to-all-start.2 = ((bf16[1,8,1,96,4,256]{5,3,1,2,0,4:T(8,128)(2,1)}), bf16[1,8,1,96,4,256]{5,3,1,2,0,4:T(8,128)(2,1)}, u32[]{:S(2)}, u32[]{:S(2)}) async-start(bf16[1,8,1,96,4,256]{5,3,1,2,0,4:T(8,128)(2,1)} %copy.24), calls=%async_computation.3 | async-start | bytes 3145728 | tf_op jit(solution)/shard_map/all_to_all | solution.py:67
  304.0 0.3 while.19
  304.4 19.8 %all-to-all-done.2 = bf16[1,8,1,96,4,256]{5,3,1,2,0,4:T(8,128)(2,1)} async-done(((bf16[1,8,1,96,4,256]{5,3,1,2,0,4:T(8,128)(2,1)}), bf16[1,8,1,96,4,256]{5,3,1,2,0,4:T(8,128)(2,1)}, u32[]{:S(2)}, u32[]{:S(2)}) %all-to-all-start.2) | async-done | bytes 1572896 | tf_op jit(solution)/shard_map/all_to_all | solution.py:67
  324.1 2.7 copy.25
  326.8 5.3 %gather_fusion.1 = bf16[1536,256]{1,0:T(8,128)(2,1)S(1)} fusion(bf16[3072,256]{1,0:T(8,128)(2,1)} %bitcast.92, s32[2048]{0:T(1024)S(1)} %pad_clamp_fusion), kind=kCustom, calls=%fused_computation.1 | custom fusion | bytes 1579008 | tf_op jit(solution)/shard_map/gather | solution.py:85
  332.1 1.9 reshape.122
  334.0 3.3 fusion.22
  337.2 1.0 fusion.12
  (31 shorter events, 0.5 us)
Async XLA Ops:
  6.5 217.4 %copy-start = (bf16[1,1024,1024]{2,1,0:T(8,128)(2,1)S(1)}, bf16[1,1024,1024]{2,1,0:T(8,128)(2,1)}, u32[]{:S(2)}) copy-start(bf16[1,1024,1024]{2,1,0:T(8,128)(2,1)} %param.13) | copy-start | bytes 6291460
  6.5 51.5 %all-gather.8.cloned.1.call-start = ((), (), s32[]{:S(2)}) async-start(), calls=%async_computation.5 | async-start | bytes 7864320 | tf_op jit(solution)/shard_map/all_gather | solution.py:50
  238.6 8.4 %copy-start.3 = (bf16[1024,32]{0,1:T(8,128)(2,1)S(1)}, bf16[1024,32]{0,1:T(8,128)(2,1)}, u32[]{:S(2)}) copy-start(bf16[1024,32]{0,1:T(8,128)(2,1)} %param.9) | copy-start | bytes 196612
  242.5 7.1 %copy-start.2 = (s32[768,2]{0,1:T(2,128)S(1)}, s32[768,2]{0,1:T(2,128)}, u32[]{:S(2)}) copy-start(s32[768,2]{0,1:T(2,128)} %param.10) | copy-start | bytes 18436
  242.5 7.2 %copy-start.4 = (s32[768]{0:T(1024)S(1)}, s32[768]{0:T(1024)}, u32[]{:S(2)}) copy-start(s32[768]{0:T(1024)} %param.11) | copy-start | bytes 9220
  242.5 54.3 %all-to-all-start.1 = ((bf16[8,1,1,96,4,256]{5,4,3,2,1,0:T(4,128)(2,1)}), bf16[8,1,1,96,4,256]{5,4,3,2,1,0:T(4,128)(2,1)}, u32[]{:S(2)}, u32[]{:S(2)}) async-start(bf16[8,1,1,96,4,256]{5,4,3,2,1,0:T(4,128)(2,1)} %bitcast.95), calls=%async_computation.2 | async-start | bytes 3145728 | tf_op jit(solution)/shard_map/all_to_all | solution.py:68
  246.9 23.3 %reduce-scatter.2.cloned.1.call-start = ((), (), s32[]{:S(2)}) async-start(), calls=%async_computation.4 | async-start | bytes 122880 | tf_op jit(solution)/shard_map/reduce_scatter | solution.py:34
  270.2 1.6 copy-start.1
  299.7 24.5 %all-to-all-start.2 = ((bf16[1,8,1,96,4,256]{5,3,1,2,0,4:T(8,128)(2,1)}), bf16[1,8,1,96,4,256]{5,3,1,2,0,4:T(8,128)(2,1)}, u32[]{:S(2)}, u32[]{:S(2)}) async-start(bf16[1,8,1,96,4,256]{5,3,1,2,0,4:T(8,128)(2,1)} %copy.24), calls=%async_computation.3 | async-start | bytes 3145728 | tf_op jit(solution)/shard_map/all_to_all | solution.py:67
Sparse Core Ops, SparseCore 0:
  8.9 49.0 all-gather.7
  250.1 19.9 reduce-scatter.1
where the time goes:
time: 346 us; the launch traced here: 345 us
  blocking collectives  160 us (46%)
  waiting for transfers between devices  72.8 us (21%)
  local copies, waits for them, and re-layouts  60 us (17%)
  matrix products  17.2 us (5%)
  between operations  13.7 us (4%)
  other arithmetic  12.8 us (4%)
  starting transfers between devices  8.8 us (3%)
    all_to_all x1, blocking collectives, per_device(): lax.all_to_all(outgoing, 'expert', split_axis=0, concat_axis=0, tiled=True)  144 us
    all_gather x1, waiting for transfers between devices, per_device(): whole_rows = lax.all_gather(samples, 'gate', axis=1, tiled=True)  31.8 us
    reduce_scatter x1, waiting for transfers between devices, per_device(): lax.psum_scatter(lax.dot_general(gate_weight, samples, (((0,), (1,)), (()...  20.5 us
    all_to_all x1, waiting for transfers between devices, per_device(): lax.all_to_all(lax.all_to_all(outbound, 'expert', split_axis=0, concat_ax...  19.8 us
    all_gather x3, blocking collectives, joined(): everything = jax.tree.map(lambda part: lax.all_gather(part, axis), shard)  15.6 us
    gather x1, local copies, waits for them, and re-layouts, per_device(): outgoing = padded[column_owners]  15.6 us
    dot_general x1, matrix products, per_device(): jnp.dot(active, down_weight[0], preferred_element_type=jnp.float32)  14.6 us
    gather x3, local copies, waits for them, and re-layouts, per_device(): jnp.take_along_axis(logits_t, jnp.clip(offset, 0, col_count - 1).T, axis=0)  9.39 us
  transfers between devices with their start and end apart: 4, of which 3 were waited for; matrix products, arithmetic and copies ran while one was open for 9% of the time, Pallas kernels for 0%

commit v1 on v0

v1 whole, which is shorter than its diff:
```python
import jax
import jax.numpy as jnp
from jax import lax
from jax.sharding import PartitionSpec as P


def peers(count, step):
    if count & (count - 1) == 0:
        return [(i, i ^ step) for i in range(count)]
    return [(i, (i + step) % count) for i in range(count)]


def owner_of(index, count, step):
    if count & (count - 1) == 0:
        return index ^ step
    return (index - step) % count


def per_device(samples, gate_weight, expert_ids, pad_mask, up_weight, down_weight):
    row_count, share = samples.shape
    group_count = lax.axis_size("expert")
    gate_count = lax.axis_size("gate")
    expert_count = group_count * gate_count
    capacity = 4 * row_count // expert_count
    gate_index = lax.axis_index("gate")

    shares = [samples]
    for step in range(1, gate_count):
        shares.append(lax.ppermute(samples, "gate", peers(gate_count, step)))

    ids = expert_ids.T
    experts = jnp.arange(expert_count, dtype=jnp.int32)
    named = ((ids[0][:, None] == experts) | (ids[1][:, None] == experts)).astype(jnp.bfloat16)
    rows = jnp.arange(row_count, dtype=jnp.int32)
    earlier = (rows[:, None] > rows[None, :]).astype(jnp.bfloat16)
    before = jnp.dot(earlier, named, preferred_element_type=jnp.float32)
    rank = jnp.sum(
        jnp.where(ids[:, :, None] == experts, before[None], 0.0), axis=2
    ).astype(jnp.int32)
    slot = ids * capacity + rank

    key = jnp.where(ids % gate_count == gate_index, ids // gate_count * capacity + rank, -1)
    column = jnp.arange(group_count * capacity, dtype=jnp.int32)[:, None]
    chooser = ((column == key[0][None, :]) | (column == key[1][None, :])).astype(jnp.bfloat16)

    partial_logits = lax.dot_general(
        gate_weight, samples, (((0,), (1,)), ((), ())), preferred_element_type=jnp.float32
    )
    logits = lax.psum(partial_logits, "gate")

    hidden = None
    for step in range(gate_count):
        outgoing = jnp.dot(
            chooser, shares[step], preferred_element_type=jnp.float32
        ).astype(jnp.bfloat16)
        incoming = lax.all_to_all(
            outgoing.reshape(group_count, capacity, share),
            "expert",
            split_axis=0,
            concat_axis=0,
            tiled=True,
        )
        weight = lax.dynamic_slice_in_dim(
            up_weight[0], owner_of(gate_index, gate_count, step) * share, share, 0
        )
        product = jnp.dot(
            incoming.reshape(group_count * capacity, share),
            weight,
            preferred_element_type=jnp.float32,
        )
        hidden = product if hidden is None else hidden + product
    active = jnp.maximum(hidden, 0.0).astype(jnp.bfloat16)
    expert_out = jnp.dot(active, down_weight[0], preferred_element_type=jnp.float32).astype(
        jnp.bfloat16
    )
    out_share = expert_out.shape[1] // gate_count
    outbound = expert_out.reshape(group_count, capacity, gate_count, out_share)
    outbound = outbound.transpose(0, 2, 1, 3).reshape(expert_count, capacity, out_share)
    returned = lax.all_to_all(
        outbound, ("expert", "gate"), split_axis=0, concat_axis=0, tiled=True
    ).reshape(expert_count * capacity, out_share)

    row_top = jnp.max(logits, axis=0)
    terms = jnp.exp(logits - row_top[None, :])
    row_total = jnp.sum(terms, axis=0)
    numerator = jnp.sum(
        jnp.where(ids[:, None, :] == experts[None, :, None], terms[None], 0.0), axis=1
    )
    factor = expert_count * numerator / row_total[None, :] * pad_mask.astype(jnp.float32)[None, :]

    every_slot = jnp.arange(expert_count * capacity, dtype=jnp.int32)
    picker = (slot.reshape(-1)[:, None] == every_slot[None, :]).astype(jnp.bfloat16)
    picked = jnp.dot(picker, returned, preferred_element_type=jnp.float32)
    mixed = factor[0][:, None] * picked[:row_count] + factor[1][:, None] * picked[row_count:]
    return mixed.astype(jnp.bfloat16)


def solution(mesh):
    placed = (
        P("expert", "gate"),
        P("gate", None),
        P("expert", None),
        P("expert"),
        P(("expert", "gate"), None, None),
        P(("expert", "gate"), None, None),
    )
    return jax.shard_map(
        per_device, mesh=mesh, in_specs=placed, out_specs=P("expert", "gate"), check_vma=False
    )
```

time: 346 us -> 263 us (0.76)
  blocking collectives: 160 us -> 0 us
  waiting for transfers between devices: 72.8 us -> 160 us
  local copies, waits for them, and re-layouts: 60 us -> 7.67 us
  matrix products: 17.2 us -> 47.4 us
  starting transfers between devices: 8.8 us -> 29 us
  other arithmetic: 12.8 us -> 4.41 us
    all_to_all x1 -> x0, blocking collectives: 144 us -> none  [per_device(): lax.all_to_all(outgoing, 'expert', split_axis=0, concat_axis=0, tiled=True)]
    ppermute x0 -> x3, waiting for transfers between devices: none -> 72 us  [per_device(): shares.append(lax.ppermute(samples, 'gate', peers(gate_count, step)))]
    dot_general x0 -> x9, matrix products: none -> 35.3 us  [the longest x3 16.7 us: per_device(): jnp.dot(incoming.reshape(group_count * capacity, share), weight, preferre...]
    psum x0 -> x1, waiting for transfers between devices: none -> 35.2 us  [per_device(): logits = lax.psum(partial_logits, 'gate')]
    all_to_all x2 -> x5, waiting for transfers between devices: 19.8 us -> 53.2 us  [the longest x4 53.2 us: per_device(): lax.all_to_all(outgoing.reshape(group_count, capacity, share), 'expert',...]
    all_gather x1 -> x0, waiting for transfers between devices: 31.8 us -> none  [per_device(): whole_rows = lax.all_gather(samples, 'gate', axis=1, tiled=True)]
    gather x5 -> x0, local copies, waits for them, and re-layouts: 30.2 us -> none  [the longest x1 15.6 us: per_device(): outgoing = padded[column_owners]]
    reduce_scatter x1 -> x0, waiting for transfers between devices: 20.5 us -> none  [per_device(): lax.psum_scatter(lax.dot_general(gate_weight, samples, (((0,), (1,)), (()...]
  transfers between devices with their start and end apart: 4 -> 9, of which waited for: 3 -> 6; matrix products, arithmetic and copies ran while one was open for 9% -> 13% of each run, Pallas kernels for 0% -> 0%
where the time goes in v1:
time: 263 us; the launch traced here: 262 us
  waiting for transfers between devices  160 us (61%)
  matrix products  47.4 us (18%)
  starting transfers between devices  29 us (11%)
  between operations  13.5 us (5%)
  local copies, waits for them, and re-layouts  7.67 us (3%)
  other arithmetic  4.41 us (2%)
    ppermute x3, waiting for transfers between devices, per_device(): shares.append(lax.ppermute(samples, 'gate', peers(gate_count, step)))  72 us
    all_to_all x4, waiting for transfers between devices, per_device(): lax.all_to_all(outgoing.reshape(group_count, capacity, share), 'expert',...  53.2 us
    psum x1, waiting for transfers between devices, per_device(): logits = lax.psum(partial_logits, 'gate')  35.2 us
    all_to_all x4, starting transfers between devices, per_device(): lax.all_to_all(outgoing.reshape(group_count, capacity, share), 'expert',...  23.4 us
    dot_general x3, matrix products, per_device(): jnp.dot(incoming.reshape(group_count * capacity, share), weight, preferre...  16.7 us
    dot_general x4, matrix products, per_device(): jnp.dot(chooser, shares[step], preferred_element_type=jnp.float32)  13.1 us
    dot_general x1, matrix products, per_device(): jnp.dot(active, down_weight[0], preferred_element_type=jnp.float32)  9.5 us
    reshape x2, local copies, waits for them, and re-layouts, per_device(): outbound = expert_out.reshape(group_count, capacity, gate_count, out_share)  6.73 us
  transfers between devices with their start and end apart: 9, of which 6 were waited for; matrix products, arithmetic and copies ran while one was open for 13% of the time, Pallas kernels for 0%

profile of v1, /device:TPU:0, one launch (start us, length us, event | category | flops | bytes accessed | tf_op | source)
XLA Modules:
  0.0 262.5 jit_solution(13644624439949326176)
XLA Ops:
  6.5 0.0 copy-start
  6.5 0.5 collective-permute-start
  7.0 0.9 slice_reduce_fusion.4
  7.9 0.7 fusion.3
  8.6 0.8 select_reduce_fusion
  9.3 0.7 convert_add_fusion
  10.1 0.3 collective-permute-done
  10.4 3.9 %convolution_convert_fusion.2 = bf16[768,1024]{1,0:T(8,128)(2,1)} fusion(bf16[768,1024]{1,0:T(8,128)(2,1)} %collective-permute-done, s32[768]{0:T(1024)S(1)} %get-tuple-element.8, s32[768]{0:T(1024)S(1)} %get-tuple-element.7), kind=kOutput, calls=%fused_computation.25 | convolution fusion | flops 1210515456 | bytes 3151872 | tf_op jit(solution)/shard_map/dot_general | solution.py:53
  14.4 7.2 %all-to-all-start.1 = ((bf16[8,96,1024]{2,1,0:T(8,128)(2,1)}), bf16[8,96,1024]{2,1,0:T(8,128)(2,1)}, u32[]{:S(2)}, u32[]{:S(2)}) async-start(bf16[8,96,1024]{2,1,0:T(8,128)(2,1)} %bitcast.50), calls=%async_computation.1 | async-start | bytes 3145728 | tf_op jit(solution)/shard_map/all_to_all | solution.py:56
  21.5 1.5 collective-permute-start.1
  23.0 34.9 %collective-permute-done.1 = bf16[768,1024]{1,0:T(8,128)(2,1)S(1)} collective-permute-done((bf16[768,1024]{1,0:T(8,128)(2,1)}, bf16[768,1024]{1,0:T(8,128)(2,1)S(1)}, u32[]{:S(2)}, u32[]{:S(2)}) %collective-permute-start.1) | collective-permute-done | bytes 1572896 | tf_op jit(solution)/shard_map/ppermute | solution.py:29
  57.9 2.6 convolution_convert_fusion.1
  60.5 0.0 all-to-all-done.1
  60.5 5.7 %all-to-all-start.2 = ((bf16[8,96,1024]{2,1,0:T(8,128)(2,1)}), bf16[8,96,1024]{2,1,0:T(8,128)(2,1)}, u32[]{:S(2)}, u32[]{:S(2)}) async-start(bf16[8,96,1024]{2,1,0:T(8,128)(2,1)} %bitcast.49), calls=%async_computation.2 | async-start | bytes 3145728 | tf_op jit(solution)/shard_map/all_to_all | solution.py:56
  66.2 0.0 collective-permute-start.2
  66.2 36.9 %collective-permute-done.2 = bf16[768,1024]{1,0:T(8,128)(2,1)S(1)} collective-permute-done((bf16[768,1024]{1,0:T(8,128)(2,1)}, bf16[768,1024]{1,0:T(8,128)(2,1)S(1)}, u32[]{:S(2)}, u32[]{:S(2)}) %collective-permute-start.2) | collective-permute-done | bytes 1572896 | tf_op jit(solution)/shard_map/ppermute | solution.py:29
  103.1 2.6 convolution_convert_fusion
  105.6 0.0 all-to-all-done.2
  105.6 6.0 %all-to-all-start.3 = ((bf16[8,96,1024]{2,1,0:T(8,128)(2,1)}), bf16[8,96,1024]{2,1,0:T(8,128)(2,1)}, u32[]{:S(2)}, u32[]{:S(2)}) async-start(bf16[8,96,1024]{2,1,0:T(8,128)(2,1)} %bitcast.51), calls=%async_computation.3 | async-start | bytes 3145728 | tf_op jit(solution)/shard_map/all_to_all | solution.py:56
  111.6 4.0 %convolution_convert_fusion.3 = bf16[768,1024]{1,0:T(8,128)(2,1)} fusion(bf16[768,1024]{1,0:T(8,128)(2,1)} %param.6, s32[768]{0:T(1024)S(1)} %get-tuple-element.8, s32[768]{0:T(1024)S(1)} %get-tuple-element.7), kind=kOutput, calls=%fused_computation.26 | convolution fusion | flops 1210515456 | bytes 3151872 | tf_op jit(solution)/shard_map/dot_general | solution.py:53
  115.6 33.4 %all-to-all-done.3 = bf16[8,96,1024]{2,1,0:T(8,128)(2,1)} async-done(((bf16[8,96,1024]{2,1,0:T(8,128)(2,1)}), bf16[8,96,1024]{2,1,0:T(8,128)(2,1)}, u32[]{:S(2)}, u32[]{:S(2)}) %all-to-all-start.3) | async-done | bytes 1572896 | tf_op jit(solution)/shard_map/all_to_all | solution.py:56
  149.0 4.5 %all-to-all-start = ((bf16[8,96,1024]{2,1,0:T(8,128)(2,1)}), bf16[8,96,1024]{2,1,0:T(8,128)(2,1)}, u32[]{:S(2)}, u32[]{:S(2)}) async-start(bf16[8,96,1024]{2,1,0:T(8,128)(2,1)} %bitcast.48), calls=%async_computation | async-start | bytes 3145728 | tf_op jit(solution)/shard_map/all_to_all | solution.py:56
  153.5 5.5 %fusion.10 = f32[768,1024]{1,0:T(8,128)} fusion(bf16[768,1024]{1,0:T(8,128)(2,1)} %bitcast.5, bf16[1,4096,1024]{2,1,0:T(8,128)(2,1)} %param.10, s32[]{:T(128)S(6)} %select_n.42), kind=kOutput, calls=%fused_computation.15 | convolution fusion | flops 1610612736 | bytes 6815748 | tf_op jit(solution)/shard_map/dot_general | solution.py:66
  159.1 5.6 %fusion.8 = f32[768,1024]{1,0:T(8,128)} fusion(bf16[768,1024]{1,0:T(8,128)(2,1)} %bitcast.8, bf16[1,4096,1024]{2,1,0:T(8,128)(2,1)} %param.10, s32[]{:T(128)S(6)} %select_n.43), kind=kOutput, calls=%fused_computation.13 | convolution fusion | flops 1610612736 | bytes 6815748 | tf_op jit(solution)/shard_map/dot_general | solution.py:66
  164.6 5.6 %fusion.6 = f32[768,1024]{1,0:T(8,128)} fusion(bf16[768,1024]{1,0:T(8,128)(2,1)} %bitcast.11, bf16[1,4096,1024]{2,1,0:T(8,128)(2,1)} %param.10, s32[]{:T(128)S(6)} %select_n.44), kind=kOutput, calls=%fused_computation.11 | convolution fusion | flops 1610612736 | bytes 6815748 | tf_op jit(solution)/shard_map/dot_general | solution.py:66
  170.2 19.8 %all-to-all-done = bf16[8,96,1024]{2,1,0:T(8,128)(2,1)} async-done(((bf16[8,96,1024]{2,1,0:T(8,128)(2,1)}), bf16[8,96,1024]{2,1,0:T(8,128)(2,1)}, u32[]{:S(2)}, u32[]{:S(2)}) %all-to-all-start) | async-done | bytes 1572896 | tf_op jit(solution)/shard_map/all_to_all | solution.py:56
  190.0 0.0 copy-done
  190.0 9.5 %fusion.18 = bf16[768,1024]{1,0:T(8,128)(2,1)} fusion(bf16[1,1024,1024]{2,1,0:T(8,128)(2,1)S(1)} %copy-done, f32[768,1024]{1,0:T(8,128)} %fusion.6, f32[768,1024]{1,0:T(8,128)} %fusion.8, f32[768,1024]{1,0:T(8,128)} %fusion.10, bf16[768,1024]{1,0:T(8,128)(2,1)} %bitcast.2, bf16[1,4096,1024]{2,1,0:T(8,128)(2,1)} %param.10, s32[]{:T(128)S(6)} %select_n.41), kind=kOutput, calls=%fused_computation.27 | convolution fusion | flops 3225944064 | bytes 16777220 | tf_op jit(solution)/shard_map/dot_general | solution.py:73
  199.5 3.9 %reshape.57 = bf16[8,96,4,256]{3,2,1,0:T(4,128)(2,1)} reshape(bf16[768,1024]{1,0:T(8,128)(2,1)} %fusion.18) | data formatting | bytes 3145728 | tf_op jit(solution)/shard_map/reshape | solution.py:77
  203.4 2.9 %copy.10 = bf16[8,96,4,256]{3,1,2,0:T(8,128)(2,1)} copy(bf16[8,96,4,256]{3,2,1,0:T(4,128)(2,1)} %reshape.57) | data formatting | bytes 3145728 | tf_op jit(solution)/shard_map/reshape | solution.py:77
  206.2 0.0 copy-start.2
  206.2 0.0 copy-start.3
  206.2 0.0 copy-start.1
  206.2 3.5 %all-to-all-start.4 = ((bf16[32,96,256]{2,1,0:T(8,128)(2,1)}), bf16[32,96,256]{2,1,0:T(8,128)(2,1)}, u32[]{:S(2)}, u32[]{:S(2)}) async-start(bf16[32,96,256]{2,1,0:T(8,128)(2,1)} %bitcast.47), calls=%async_computation.4 | async-start | bytes 3145728 | tf_op jit(solution)/shard_map/all_to_all | solution.py:79
  209.8 0.0 all-reduce.2.cloned.1.call-start
  209.8 0.0 copy-done.2
  209.9 2.6 %fusion.43 = f32[32,768]{1,0:T(8,128)} fusion(bf16[1024,32]{0,1:T(8,128)(2,1)S(1)} %copy-done.2, bf16[768,1024]{1,0:T(8,128)(2,1)} %param.6), kind=kOutput, calls=%fused_computation.63 | convolution fusion | flops 50331648 | bytes 1736704 | tf_op jit(solution)/shard_map/dot_general | solution.py:46
  212.5 0.0 all-reduce.2.cloned.1.call-update
  212.5 0.0 copy-done.3
  212.5 35.2 %all-reduce.2.cloned.1.call-done = f32[32,768]{1,0:T(8,128)} async-done(((f32[32,768]{1,0:T(8,128)}), f32[32,768]{1,0:T(8,128)}) %all-reduce.2.cloned.1.call-update) | async-done | bytes 98320 | tf_op jit(solution)/shard_map/psum | solution.py:49
  247.7 0.9 reduce_max.9
  248.6 0.9 fusion.42
  249.6 0.0 copy-done.1
  249.7 0.0 all-to-all-done.4
  249.7 4.9 %fusion = f32[1536,256]{1,0:T(8,128)S(1)} fusion(bf16[3072,256]{1,0:T(8,128)(2,1)} %bitcast.16, s32[1536]{0:T(1024)S(1)} %eq.119), kind=kOutput, calls=%fused_computation.1 | convolution fusion | flops 2420637696 | bytes 3151872 | tf_op jit(solution)/shard_map/dot_general | solution.py:93
  254.6 1.0 fusion.31
  (6 shorter events, 0.1 us)
Async XLA Ops:
  6.5 183.5 %copy-start = (bf16[1,1024,1024]{2,1,0:T(8,128)(2,1)S(1)}, bf16[1,1024,1024]{2,1,0:T(8,128)(2,1)}, u32[]{:S(2)}) copy-start(bf16[1,1024,1024]{2,1,0:T(8,128)(2,1)} %param.11) | copy-start | bytes 6291460
  6.5 3.9 %collective-permute-start = (bf16[768,1024]{1,0:T(8,128)(2,1)}, bf16[768,1024]{1,0:T(8,128)(2,1)}, u32[]{:S(2)}, u32[]{:S(2)}) collective-permute-start(bf16[768,1024]{1,0:T(8,128)(2,1)} %param.6), channel_id=1, source_target_pairs={{0,1},{1,0},{2,3},{3,2},{4,5},{5,4},{6,7},{7,6},{8,9},{9,8},{10,11... | collective-permute-start | bytes 4718600 | tf_op jit(solution)/shard_map/ppermute | solution.py:29
  14.4 46.1 %all-to-all-start.1 = ((bf16[8,96,1024]{2,1,0:T(8,128)(2,1)}), bf16[8,96,1024]{2,1,0:T(8,128)(2,1)}, u32[]{:S(2)}, u32[]{:S(2)}) async-start(bf16[8,96,1024]{2,1,0:T(8,128)(2,1)} %bitcast.50), calls=%async_computation.1 | async-start | bytes 3145728 | tf_op jit(solution)/shard_map/all_to_all | solution.py:56
  21.5 36.4 %collective-permute-start.1 = (bf16[768,1024]{1,0:T(8,128)(2,1)}, bf16[768,1024]{1,0:T(8,128)(2,1)S(1)}, u32[]{:S(2)}, u32[]{:S(2)}) collective-permute-start(bf16[768,1024]{1,0:T(8,128)(2,1)} %param.6), channel_id=1, source_target_pairs={{0,2},{1,3},{2,0},{3,1},{4,6},{5,7},{6,4},{7,5},{8,10},{9,11},{10,... | collective-permute-start | bytes 4718600 | tf_op jit(solution)/shard_map/ppermute | solution.py:29
  60.5 45.2 %all-to-all-start.2 = ((bf16[8,96,1024]{2,1,0:T(8,128)(2,1)}), bf16[8,96,1024]{2,1,0:T(8,128)(2,1)}, u32[]{:S(2)}, u32[]{:S(2)}) async-start(bf16[8,96,1024]{2,1,0:T(8,128)(2,1)} %bitcast.49), calls=%async_computation.2 | async-start | bytes 3145728 | tf_op jit(solution)/shard_map/all_to_all | solution.py:56
  66.2 36.9 %collective-permute-start.2 = (bf16[768,1024]{1,0:T(8,128)(2,1)}, bf16[768,1024]{1,0:T(8,128)(2,1)S(1)}, u32[]{:S(2)}, u32[]{:S(2)}) collective-permute-start(bf16[768,1024]{1,0:T(8,128)(2,1)} %param.6), channel_id=1, source_target_pairs={{0,3},{1,2},{2,1},{3,0},{4,7},{5,6},{6,5},{7,4},{8,11},{9,10},{10,... | collective-permute-start | bytes 4718600 | tf_op jit(solution)/shard_map/ppermute | solution.py:29
  105.6 43.4 %all-to-all-start.3 = ((bf16[8,96,1024]{2,1,0:T(8,128)(2,1)}), bf16[8,96,1024]{2,1,0:T(8,128)(2,1)}, u32[]{:S(2)}, u32[]{:S(2)}) async-start(bf16[8,96,1024]{2,1,0:T(8,128)(2,1)} %bitcast.51), calls=%async_computation.3 | async-start | bytes 3145728 | tf_op jit(solution)/shard_map/all_to_all | solution.py:56
  149.0 41.0 %all-to-all-start = ((bf16[8,96,1024]{2,1,0:T(8,128)(2,1)}), bf16[8,96,1024]{2,1,0:T(8,128)(2,1)}, u32[]{:S(2)}, u32[]{:S(2)}) async-start(bf16[8,96,1024]{2,1,0:T(8,128)(2,1)} %bitcast.48), calls=%async_computation | async-start | bytes 3145728 | tf_op jit(solution)/shard_map/all_to_all | solution.py:56
  206.2 3.6 %copy-start.2 = (bf16[1024,32]{0,1:T(8,128)(2,1)S(1)}, bf16[1024,32]{0,1:T(8,128)(2,1)}, u32[]{:S(2)}) copy-start(bf16[1024,32]{0,1:T(8,128)(2,1)} %param.7) | copy-start | bytes 196612
  206.2 6.3 %copy-start.3 = (s32[768]{0:T(1024)S(1)}, s32[768]{0:T(1024)}, u32[]{:S(2)}) copy-start(s32[768]{0:T(1024)} %param.9) | copy-start | bytes 9220
  206.2 43.3 %copy-start.1 = (s32[768,2]{0,1:T(2,128)S(1)}, s32[768,2]{0,1:T(2,128)}, u32[]{:S(2)}) copy-start(s32[768,2]{0,1:T(2,128)} %param.8) | copy-start | bytes 18436
  206.2 43.4 %all-to-all-start.4 = ((bf16[32,96,256]{2,1,0:T(8,128)(2,1)}), bf16[32,96,256]{2,1,0:T(8,128)(2,1)}, u32[]{:S(2)}, u32[]{:S(2)}) async-start(bf16[32,96,256]{2,1,0:T(8,128)(2,1)} %bitcast.47), calls=%async_computation.4 | async-start | bytes 3145728 | tf_op jit(solution)/shard_map/all_to_all | solution.py:79
  209.8 37.9 %all-reduce.2.cloned.1.call-start = ((), (), s32[]{:S(2)}) async-start(), calls=%async_computation.5 | async-start | bytes 196608 | tf_op jit(solution)/shard_map/psum | solution.py:49
Sparse Core Ops, SparseCore 0:
  212.9 34.7 all-reduce.1

commit v2 on v1

--- a/solution.py
+++ b/solution.py
@@ -37,7 +37,7 @@
     rank = jnp.sum(
         jnp.where(ids[:, :, None] == experts, before[None], 0.0), axis=2
     ).astype(jnp.int32)
-    slot = ids * capacity + rank
+    slot = (ids % gate_count * group_count + ids // gate_count) * capacity + rank
 
     key = jnp.where(ids % gate_count == gate_index, ids // gate_count * capacity + rank, -1)
     column = jnp.arange(group_count * capacity, dtype=jnp.int32)[:, None]
@@ -48,36 +48,46 @@
     )
     logits = lax.psum(partial_logits, "gate")
 
+    chooser = lax.optimization_barrier(chooser)
+    stages = stages_of(gate_count)
     hidden = None
-    for step in range(gate_count):
-        outgoing = jnp.dot(
-            chooser, shares[step], preferred_element_type=jnp.float32
-        ).astype(jnp.bfloat16)
+    for stage, steps in enumerate(stages):
+        picks = [
+            jnp.dot(chooser, shares[step], preferred_element_type=jnp.float32)
+            .astype(jnp.bfloat16)
+            .reshape(group_count, 1, capacity, share)
+            for step in steps
+        ]
+        outgoing = picks[0] if len(steps) == 1 else jnp.concatenate(picks, axis=1)
         incoming = lax.all_to_all(
-            outgoing.reshape(group_count, capacity, share),
-            "expert",
-            split_axis=0,
-            concat_axis=0,
-            tiled=True,
+            outgoing, "expert", split_axis=0, concat_axis=0, tiled=True
         )
-        weight = lax.dynamic_slice_in_dim(
-            up_weight[0], owner_of(gate_index, gate_count, step) * share, share, 0
-        )
-        product = jnp.dot(
-            incoming.reshape(group_count * capacity, share),
-            weight,
-            preferred_element_type=jnp.float32,
-        )
-        hidden = product if hidden is None else hidden + product
+        for place, step in enumerate(steps):
+            weight = lax.dynamic_slice_in_dim(
+                up_weight[0], owner_of(gate_index, gate_count, step) * share, share, 0
+            )
+            product = jnp.dot(
+                incoming[:, place].reshape(group_count * capacity, share),
+                weight,
+                preferred_element_type=jnp.float32,
+            )
+            hidden = product if hidden is None else hidden + product
+        if stage + 1 < len(stages):
+            hidden = lax.optimization_barrier(hidden)
     active = jnp.maximum(hidden, 0.0).astype(jnp.bfloat16)
-    expert_out = jnp.dot(active, down_weight[0], preferred_element_type=jnp.float32).astype(
-        jnp.bfloat16
-    )
-    out_share = expert_out.shape[1] // gate_count
-    outbound = expert_out.reshape(group_count, capacity, gate_count, out_share)
-    outbound = outbound.transpose(0, 2, 1, 3).reshape(expert_count, capacity, out_share)
+    out_share = down_weight.shape[2] // gate_count
+    outbound = jnp.stack(
+        [
+            jnp.dot(
+                active,
+                down_weight[0, :, part * out_share : (part + 1) * out_share],
+                preferred_element_type=jnp.float32,
+            ).astype(jnp.bfloat16)
+            for part in range(gate_count)
+        ]
+    ).reshape(expert_count, capacity, out_share)
     returned = lax.all_to_all(
-        outbound, ("expert", "gate"), split_axis=0, concat_axis=0, tiled=True
+        outbound, ("gate", "expert"), split_axis=0, concat_axis=0, tiled=True
     ).reshape(expert_count * capacity, out_share)
 
     row_top = jnp.max(logits, axis=0)
@@ -95,6 +105,12 @@
     return mixed.astype(jnp.bfloat16)
 
 
+def stages_of(gate_count):
+    if gate_count < 4:
+        return [[step] for step in range(gate_count)]
+    return [[0], list(range(1, gate_count - 1)), [gate_count - 1]]
+
+
 def solution(mesh):
     placed = (
         P("expert", "gate"),

time: 263 us -> 242 us (0.920)
  matrix products: 47.4 us -> 32.8 us
  starting transfers between devices: 29 us -> 23.5 us
  local copies, waits for them, and re-layouts: 7.67 us -> 2.45 us
  other arithmetic: 4.41 us -> 9.12 us
    dot_general x4 -> x8, matrix products: 26.2 us -> 17 us  [the longest x4 14.7 us: per_device(): jnp.dot(incoming[:, place].reshape(group_count * capacity, share), weight...]
    reshape x2 -> x0, local copies, waits for them, and re-layouts: 6.73 us -> none  [per_device(): outbound = expert_out.reshape(group_count, capacity, gate_count, out_share)]
    all_to_all x5 -> x4, starting transfers between devices: 27 us -> 21.2 us  [the longest x3 17.7 us: per_device(): lax.all_to_all(outgoing, 'expert', split_axis=0, concat_axis=0, tiled=True)]
    ppermute x3, waiting for transfers between devices: 72 us -> 69 us  [per_device(): shares.append(lax.ppermute(samples, 'gate', peers(gate_count, step)))]
    dot_general x4, matrix products: 13.1 us -> 10.4 us  [per_device(): jnp.dot(chooser, shares[step], preferred_element_type=jnp.float32)]
    all_to_all x5 -> x4, waiting for transfers between devices: 53.2 us -> 55.2 us  [the longest x3 55.2 us: per_device(): lax.all_to_all(outgoing, 'expert', split_axis=0, concat_axis=0, tiled=True)]
  transfers between devices with their start and end apart: 9 -> 8, of which waited for: 6 -> 6; matrix products, arithmetic and copies ran while one was open for 13% -> 10% of each run, Pallas kernels for 0% -> 0%
where the time goes in v2:
time: 242 us; the launch traced here: 241 us
  waiting for transfers between devices  160 us (66%)
  matrix products  32.8 us (14%)
  starting transfers between devices  23.5 us (10%)
  between operations  13.7 us (6%)
  other arithmetic  9.12 us (4%)
  local copies, waits for them, and re-layouts  2.45 us (1%)
    ppermute x3, waiting for transfers between devices, per_device(): shares.append(lax.ppermute(samples, 'gate', peers(gate_count, step)))  69 us
    all_to_all x3, waiting for transfers between devices, per_device(): lax.all_to_all(outgoing, 'expert', split_axis=0, concat_axis=0, tiled=True)  55.2 us
    psum x1, waiting for transfers between devices, per_device(): logits = lax.psum(partial_logits, 'gate')  35.3 us
    all_to_all x3, starting transfers between devices, per_device(): lax.all_to_all(outgoing, 'expert', split_axis=0, concat_axis=0, tiled=True)  17.7 us
    dot_general x4, matrix products, per_device(): jnp.dot(incoming[:, place].reshape(group_count * capacity, share), weight...  14.7 us
    dot_general x4, matrix products, per_device(): jnp.dot(chooser, shares[step], preferred_element_type=jnp.float32)  10.4 us
  transfers between devices with their start and end apart: 8, of which 6 were waited for; matrix products, arithmetic and copies ran while one was open for 10% of the time, Pallas kernels for 0%

profile of v2, /device:TPU:0, one launch (start us, length us, event | category | flops | bytes accessed | tf_op | source)
XLA Modules:
  0.0 241.2 jit_solution(16256547052824188166)
XLA Ops:
  6.5 0.0 copy-start
  6.5 0.0 copy-start.2
  6.5 0.9 slice_reduce_fusion.4
  7.4 0.7 fusion.4
  8.1 0.8 select_reduce_fusion
  8.8 0.7 convert_add_fusion
  9.6 0.7 compare_select_fusion
  10.3 0.7 fusion.3
  11.0 0.0 copy-done.2
  11.0 0.0 copy-start.4
  11.0 2.5 %convolution_convert_fusion.3 = bf16[768,1024]{1,0:T(8,128)(2,1)} fusion(bf16[768,768]{1,0:T(8,128)(2,1)S(1)} %fusion.3, bf16[768,1024]{1,0:T(8,128)(2,1)S(1)} %copy-done.2), kind=kOutput, calls=%fused_computation.27 | convolution fusion | flops 1208745984 | bytes 4325376 | tf_op jit(solution)/shard_map/dot_general | solution.py:56
  13.6 0.0 copy-done.4
  13.6 7.3 %all-to-all-start = ((bf16[8,1,96,1024]{3,2,1,0:T(8,128)(2,1)}), bf16[8,1,96,1024]{3,2,1,0:T(8,128)(2,1)S(1)}, u32[]{:S(2)}, u32[]{:S(2)}) async-start(bf16[8,1,96,1024]{3,2,1,0:T(8,128)(2,1)} %bitcast.2), calls=%async_computation | async-start | bytes 3145728 | tf_op jit(solution)/shard_map/all_to_all | solution.py:62
  20.9 0.0 copy-start.5
  20.9 0.1 collective-permute-start
  21.0 1.6 collective-permute-start.1
  22.5 1.8 collective-permute-done
  24.4 2.7 %convolution_convert_fusion.2 = bf16[768,1024]{1,0:T(8,128)(2,1)S(1)} fusion(bf16[768,768]{1,0:T(8,128)(2,1)} %copy-done.4, bf16[768,1024]{1,0:T(8,128)(2,1)S(1)} %collective-permute-done), kind=kOutput, calls=%fused_computation.26 | convolution fusion | flops 1208745984 | bytes 4325376 | tf_op jit(solution)/shard_map/dot_general | solution.py:56
  27.0 30.7 %collective-permute-done.1 = bf16[768,1024]{1,0:T(8,128)(2,1)S(1)} collective-permute-done((bf16[768,1024]{1,0:T(8,128)(2,1)S(1)}, bf16[768,1024]{1,0:T(8,128)(2,1)S(1)}, u32[]{:S(2)}, u32[]{:S(2)}) %collective-permute-start.1) | collective-permute-done | bytes 1572896 | tf_op jit(solution)/shard_map/ppermute | solution.py:29
  57.8 0.0 copy-done.5
  57.8 1.4 convolution_convert_fusion.1
  59.2 2.0 pad_maximum_fusion
  61.1 0.0 all-to-all-done
  61.1 0.0 copy-start.1
  61.1 1.1 copy-done.1
  62.2 5.9 %all-to-all-start.1 = ((bf16[8,2,96,1024]{3,2,1,0:T(8,128)(2,1)}), bf16[8,2,96,1024]{3,2,1,0:T(8,128)(2,1)S(1)}, u32[]{:S(2)}, u32[]{:S(2)}) async-start(bf16[8,2,96,1024]{3,2,1,0:T(8,128)(2,1)} %pad_maximum_fusion), calls=%async_computation.1 | async-start | bytes 6291456 | tf_op jit(solution)/shard_map/all_to_all | solution.py:62
  68.2 0.4 collective-permute-start.2
  68.6 36.5 %collective-permute-done.2 = bf16[768,1024]{1,0:T(8,128)(2,1)S(1)} collective-permute-done((bf16[768,1024]{1,0:T(8,128)(2,1)}, bf16[768,1024]{1,0:T(8,128)(2,1)S(1)}, u32[]{:S(2)}, u32[]{:S(2)}) %collective-permute-start.2) | collective-permute-done | bytes 1572896 | tf_op jit(solution)/shard_map/ppermute | solution.py:29
  105.0 3.8 %convolution_convert_fusion = bf16[768,1024]{1,0:T(8,128)(2,1)} fusion(bf16[768,768]{1,0:T(8,128)(2,1)} %copy-done.4, bf16[768,1024]{1,0:T(8,128)(2,1)S(1)} %collective-permute-done.2), kind=kOutput, calls=%fused_computation.24 | convolution fusion | flops 1208745984 | bytes 4325376 | tf_op jit(solution)/shard_map/dot_general | solution.py:56
  108.9 29.8 %all-to-all-done.1 = bf16[8,2,96,1024]{3,2,1,0:T(8,128)(2,1)S(1)} async-done(((bf16[8,2,96,1024]{3,2,1,0:T(8,128)(2,1)}), bf16[8,2,96,1024]{3,2,1,0:T(8,128)(2,1)S(1)}, u32[]{:S(2)}, u32[]{:S(2)}) %all-to-all-start.1) | async-done | bytes 3145760 | tf_op jit(solution)/shard_map/all_to_all | solution.py:62
  138.6 4.5 %all-to-all-start.2 = ((bf16[8,1,96,1024]{3,2,1,0:T(8,128)(2,1)}), bf16[8,1,96,1024]{3,2,1,0:T(8,128)(2,1)}, u32[]{:S(2)}, u32[]{:S(2)}) async-start(bf16[8,1,96,1024]{3,2,1,0:T(8,128)(2,1)} %bitcast.86), calls=%async_computation.2 | async-start | bytes 3145728 | tf_op jit(solution)/shard_map/all_to_all | solution.py:62
  143.1 3.9 %fusion.11 = f32[768,1024]{1,0:T(8,128)S(1)} fusion(bf16[768,1024]{1,0:T(8,128)(2,1)} %bitcast.85, bf16[1,4096,1024]{2,1,0:T(8,128)(2,1)} %param.10, s32[]{:T(128)S(6)} %select_n.44), kind=kOutput, calls=%fused_computation.18 | convolution fusion | flops 1610612736 | bytes 6815748 | tf_op jit(solution)/shard_map/dot_general | solution.py:69
  147.0 0.4 fusion.44
  147.4 3.4 %fusion.7 = f32[768,1024]{1,0:T(8,128)S(1)} fusion(bf16[768,1024]{1,0:T(8,128)(2,1)S(1)} %bitcast.90, bf16[1,4096,1024]{2,1,0:T(8,128)(2,1)} %param.10, s32[]{:T(128)S(6)} %select_n.46), kind=kOutput, calls=%fused_computation.14 | convolution fusion | flops 1610612736 | bytes 6815748 | tf_op jit(solution)/shard_map/dot_general | solution.py:69
  150.8 3.4 %add_add_fusion = f32[768,1024]{1,0:T(8,128)S(1)} fusion(f32[768,1024]{1,0:T(8,128)S(1)} %fusion.7, f32[768,1024]{1,0:T(8,128)S(1)} %fusion.11, bf16[768,1024]{1,0:T(8,128)(2,1)S(1)} %bitcast.88, bf16[1,4096,1024]{2,1,0:T(8,128)(2,1)} %param.10, s32[]{:T(128)S(6)} %select_n.45), kind=kOutput, calls=%fused_computation.5 | convolution fusion | flops 1612185600 | bytes 13107204 | tf_op jit(solution)/shard_map/dot_general | solution.py:69
  154.2 25.4 %all-to-all-done.2 = bf16[8,1,96,1024]{3,2,1,0:T(8,128)(2,1)} async-done(((bf16[8,1,96,1024]{3,2,1,0:T(8,128)(2,1)}), bf16[8,1,96,1024]{3,2,1,0:T(8,128)(2,1)}, u32[]{:S(2)}, u32[]{:S(2)}) %all-to-all-start.2) | async-done | bytes 1572896 | tf_op jit(solution)/shard_map/all_to_all | solution.py:62
  179.7 0.0 copy-start.8
  179.7 4.0 %maximum_convert_fusion = bf16[768,1024]{1,0:T(8,128)(2,1)S(1)} fusion(f32[768,1024]{1,0:T(8,128)S(1)} %add_add_fusion, bf16[768,1024]{1,0:T(8,128)(2,1)} %bitcast.15, bf16[1,4096,1024]{2,1,0:T(8,128)(2,1)} %param.10, s32[]{:T(128)S(6)} %select_n.47), kind=kOutput, calls=%fused_computation.4 | convolution fusion | flops 1612972032 | bytes 8388612 | tf_op jit(solution)/shard_map/dot_general | solution.py:69
  183.7 0.0 copy-done.8
  183.7 0.6 fusion.21
  184.3 0.6 fusion.22
  184.9 0.6 fusion.23
  185.5 0.6 fusion.24
  186.0 1.4 pad_maximum_fusion.1
  187.4 0.0 copy-start.3
  187.4 3.5 %all-to-all-start.3 = ((bf16[32,96,256]{2,1,0:T(8,128)(2,1)}), bf16[32,96,256]{2,1,0:T(8,128)(2,1)S(1)}, u32[]{:S(2)}, u32[]{:S(2)}) async-start(bf16[32,96,256]{2,1,0:T(8,128)(2,1)} %bitcast.25), calls=%async_computation.3 | async-start | bytes 3145728 | tf_op jit(solution)/shard_map/all_to_all | solution.py:89
  190.9 0.0 copy-start.7
  191.0 0.0 copy-start.6
  191.0 0.3 all-reduce.2.cloned.1.call-start
  191.2 0.0 copy-done
  191.2 0.0 copy-done.3
  191.3 1.2 fusion.45
  192.5 0.0 all-reduce.2.cloned.1.call-update
  192.5 0.0 copy-done.7
  192.5 35.3 %all-reduce.2.cloned.1.call-done = f32[32,768]{1,0:T(8,128)} async-done(((f32[32,768]{1,0:T(8,128)}), f32[32,768]{1,0:T(8,128)}) %all-reduce.2.cloned.1.call-update) | async-done | bytes 98320 | tf_op jit(solution)/shard_map/psum | solution.py:49
  227.8 0.9 reduce_max.9
  228.8 0.9 fusion.43
  229.7 0.0 copy-done.6
  229.8 0.0 all-to-all-done.3
  229.8 3.5 %fusion = f32[1536,256]{1,0:T(8,128)S(1)} fusion(bf16[3072,256]{1,0:T(8,128)(2,1)S(1)} %bitcast.87, s32[1536]{0:T(1024)S(1)} %eq.120), kind=kOutput, calls=%fused_computation.1 | convolution fusion | flops 2420637696 | bytes 3151872 | tf_op jit(solution)/shard_map/dot_general | solution.py:103
  233.3 1.0 fusion.26
  (6 shorter events, 0.1 us)
Async XLA Ops:
  6.5 184.7 %copy-start = (bf16[1024,32]{0,1:T(8,128)(2,1)S(1)}, bf16[1024,32]{0,1:T(8,128)(2,1)}, u32[]{:S(2)}) copy-start(bf16[1024,32]{0,1:T(8,128)(2,1)} %param.7) | copy-start | bytes 196612
  6.5 4.5 %copy-start.2 = (bf16[768,1024]{1,0:T(8,128)(2,1)S(1)}, bf16[768,1024]{1,0:T(8,128)(2,1)}, u32[]{:S(2)}) copy-start(bf16[768,1024]{1,0:T(8,128)(2,1)} %param.6) | copy-start | bytes 4718596
  11.0 2.5 %copy-start.4 = (bf16[768,768]{1,0:T(8,128)(2,1)}, bf16[768,768]{1,0:T(8,128)(2,1)S(1)}, u32[]{:S(2)}) copy-start(bf16[768,768]{1,0:T(8,128)(2,1)S(1)} %fusion.3) | copy-start | bytes 3538948
  13.6 47.5 %all-to-all-start = ((bf16[8,1,96,1024]{3,2,1,0:T(8,128)(2,1)}), bf16[8,1,96,1024]{3,2,1,0:T(8,128)(2,1)S(1)}, u32[]{:S(2)}, u32[]{:S(2)}) async-start(bf16[8,1,96,1024]{3,2,1,0:T(8,128)(2,1)} %bitcast.2), calls=%async_computation | async-start | bytes 3145728 | tf_op jit(solution)/shard_map/all_to_all | solution.py:62
  20.9 36.9 %copy-start.5 = (bf16[768,768]{1,0:T(8,128)(2,1)S(1)}, bf16[768,768]{1,0:T(8,128)(2,1)}, u32[]{:S(2)}) copy-start(bf16[768,768]{1,0:T(8,128)(2,1)} %copy-done.4) | copy-start | bytes 3538948
  20.9 3.5 %collective-permute-start = (bf16[768,1024]{1,0:T(8,128)(2,1)S(1)}, bf16[768,1024]{1,0:T(8,128)(2,1)S(1)}, u32[]{:S(2)}, u32[]{:S(2)}) collective-permute-start(bf16[768,1024]{1,0:T(8,128)(2,1)S(1)} %copy-done.2), channel_id=1, source_target_pairs={{0,1},{1,0},{2,3},{3,2},{4,5},{5,4},{6,7},{7,6},{8,9},{9,8},{10,11... | collective-permute-start | bytes 4718600 | tf_op jit(solution)/shard_map/ppermute | solution.py:29
  21.0 36.8 %collective-permute-start.1 = (bf16[768,1024]{1,0:T(8,128)(2,1)S(1)}, bf16[768,1024]{1,0:T(8,128)(2,1)S(1)}, u32[]{:S(2)}, u32[]{:S(2)}) collective-permute-start(bf16[768,1024]{1,0:T(8,128)(2,1)S(1)} %copy-done.2), channel_id=1, source_target_pairs={{0,2},{1,3},{2,0},{3,1},{4,6},{5,7},{6,4},{7,5},{8,10},{9,11},{10,... | collective-permute-start | bytes 4718600 | tf_op jit(solution)/shard_map/ppermute | solution.py:29
  61.1 1.1 copy-start.1
  62.2 76.4 %all-to-all-start.1 = ((bf16[8,2,96,1024]{3,2,1,0:T(8,128)(2,1)}), bf16[8,2,96,1024]{3,2,1,0:T(8,128)(2,1)S(1)}, u32[]{:S(2)}, u32[]{:S(2)}) async-start(bf16[8,2,96,1024]{3,2,1,0:T(8,128)(2,1)} %pad_maximum_fusion), calls=%async_computation.1 | async-start | bytes 6291456 | tf_op jit(solution)/shard_map/all_to_all | solution.py:62
  68.2 36.9 %collective-permute-start.2 = (bf16[768,1024]{1,0:T(8,128)(2,1)}, bf16[768,1024]{1,0:T(8,128)(2,1)S(1)}, u32[]{:S(2)}, u32[]{:S(2)}) collective-permute-start(bf16[768,1024]{1,0:T(8,128)(2,1)} %param.6), channel_id=1, source_target_pairs={{0,3},{1,2},{2,1},{3,0},{4,7},{5,6},{6,5},{7,4},{8,11},{9,10},{10,... | collective-permute-start | bytes 4718600 | tf_op jit(solution)/shard_map/ppermute | solution.py:29
  138.6 41.0 %all-to-all-start.2 = ((bf16[8,1,96,1024]{3,2,1,0:T(8,128)(2,1)}), bf16[8,1,96,1024]{3,2,1,0:T(8,128)(2,1)}, u32[]{:S(2)}, u32[]{:S(2)}) async-start(bf16[8,1,96,1024]{3,2,1,0:T(8,128)(2,1)} %bitcast.86), calls=%async_computation.2 | async-start | bytes 3145728 | tf_op jit(solution)/shard_map/all_to_all | solution.py:62
  179.7 4.0 %copy-start.8 = (bf16[1,1024,1024]{2,1,0:T(8,128)(2,1)S(1)}, bf16[1,1024,1024]{2,1,0:T(8,128)(2,1)}, u32[]{:S(2)}) copy-start(bf16[1,1024,1024]{2,1,0:T(8,128)(2,1)} %param.11) | copy-start | bytes 6291460
  187.4 3.9 %copy-start.3 = (bf16[768,1024]{1,0:T(8,128)(2,1)S(1)}, bf16[768,1024]{1,0:T(8,128)(2,1)}, u32[]{:S(2)}) copy-start(bf16[768,1024]{1,0:T(8,128)(2,1)} %param.6) | copy-start | bytes 4718596
  187.4 42.4 %all-to-all-start.3 = ((bf16[32,96,256]{2,1,0:T(8,128)(2,1)}), bf16[32,96,256]{2,1,0:T(8,128)(2,1)S(1)}, u32[]{:S(2)}, u32[]{:S(2)}) async-start(bf16[32,96,256]{2,1,0:T(8,128)(2,1)} %bitcast.25), calls=%async_computation.3 | async-start | bytes 3145728 | tf_op jit(solution)/shard_map/all_to_all | solution.py:89
  190.9 1.6 copy-start.7
  191.0 38.7 %copy-start.6 = (s32[768,2]{0,1:T(2,128)S(1)}, s32[768,2]{0,1:T(2,128)}, u32[]{:S(2)}) copy-start(s32[768,2]{0,1:T(2,128)} %param.8) | copy-start | bytes 18436
  191.0 36.9 %all-reduce.2.cloned.1.call-start = ((), (), s32[]{:S(2)}) async-start(), calls=%async_computation.4 | async-start | bytes 196608 | tf_op jit(solution)/shard_map/psum | solution.py:49
Sparse Core Ops, SparseCore 0:
  194.1 33.7 all-reduce.1

commit v3 on v2

--- a/solution.py
+++ b/solution.py
@@ -14,6 +14,24 @@
     if count & (count - 1) == 0:
         return index ^ step
     return (index - step) % count
+
+
+def hopped(turned, rows, group_count, capacity):
+    own = lax.axis_index("expert")
+    arrived = []
+    for hop in range(group_count):
+        piece = jnp.dot(
+            turned[hop * capacity : (hop + 1) * capacity],
+            rows,
+            preferred_element_type=jnp.float32,
+        ).astype(jnp.bfloat16)
+        if hop:
+            links = [(i, (i + hop) % group_count) for i in range(group_count)]
+            piece = lax.ppermute(piece, "expert", links)
+        arrived.append(piece)
+    listed = [arrived[-place % group_count] for place in range(group_count)]
+    twice = jnp.stack(listed + listed)
+    return lax.dynamic_slice_in_dim(twice, group_count - own, group_count, 0)
 
 
 def per_device(samples, gate_weight, expert_ids, pad_mask, up_weight, down_weight):
@@ -48,20 +66,30 @@
     )
     logits = lax.psum(partial_logits, "gate")
 
-    chooser = lax.optimization_barrier(chooser)
+    own = lax.axis_index("expert")
+    ahead = jnp.where(
+        ids % gate_count == gate_index,
+        (ids // gate_count - own) % group_count * capacity + rank,
+        -1,
+    )
+    turned = ((column == ahead[0][None, :]) | (column == ahead[1][None, :])).astype(jnp.bfloat16)
+    chooser, turned = lax.optimization_barrier((chooser, turned))
     stages = stages_of(gate_count)
     hidden = None
     for stage, steps in enumerate(stages):
-        picks = [
-            jnp.dot(chooser, shares[step], preferred_element_type=jnp.float32)
-            .astype(jnp.bfloat16)
-            .reshape(group_count, 1, capacity, share)
-            for step in steps
-        ]
-        outgoing = picks[0] if len(steps) == 1 else jnp.concatenate(picks, axis=1)
-        incoming = lax.all_to_all(
-            outgoing, "expert", split_axis=0, concat_axis=0, tiled=True
-        )
+        if 0 < stage < len(stages) - 1:
+            incoming = jnp.stack(
+                [hopped(turned, shares[step], group_count, capacity) for step in steps], axis=1
+            )
+        else:
+            picks = [
+                jnp.dot(chooser, shares[step], preferred_element_type=jnp.float32)
+                .astype(jnp.bfloat16)
+                .reshape(group_count, 1, capacity, share)
+                for step in steps
+            ]
+            outgoing = picks[0] if len(steps) == 1 else jnp.concatenate(picks, axis=1)
+            incoming = lax.all_to_all(outgoing, "expert", split_axis=0, concat_axis=0, tiled=True)
         for place, step in enumerate(steps):
             weight = lax.dynamic_slice_in_dim(
                 up_weight[0], owner_of(gate_index, gate_count, step) * share, share, 0

time: 242 us -> 246 us (1.017)
  waiting for transfers between devices: 160 us -> 110 us
  starting transfers between devices: 23.5 us -> 49.9 us
  local copies, waits for them, and re-layouts: 2.45 us -> 25 us
  matrix products: 32.8 us -> 38.5 us
    all_to_all x3 -> x2, waiting for transfers between devices: 55.2 us -> 20.1 us  [per_device(): lax.all_to_all(outgoing, 'expert', split_axis=0, concat_axis=0, tiled=True)]
    ppermute x3, waiting for transfers between devices: 69 us -> 34.4 us  [per_device(): shares.append(lax.ppermute(samples, 'gate', peers(gate_count, step)))]
    ppermute x0 -> x14, starting transfers between devices: none -> 32.7 us  [hopped(): piece = lax.ppermute(piece, 'expert', links)]
    ppermute x0 -> x14, waiting for transfers between devices: none -> 19.8 us  [hopped(): piece = lax.ppermute(piece, 'expert', links)]
    unnamed x18 -> x50, local copies, waits for them, and re-layouts: 1.17 us -> 19.5 us
    dot_general x0 -> x16, matrix products: none -> 9.53 us  [hopped(): jnp.dot(turned[hop * capacity:(hop + 1) * capacity], rows, preferred_elem...]
    all_to_all x3 -> x2, starting transfers between devices: 17.7 us -> 10.1 us  [per_device(): lax.all_to_all(outgoing, 'expert', split_axis=0, concat_axis=0, tiled=True)]
    dot_general x4 -> x2, matrix products: 10.4 us -> 6.59 us  [per_device(): jnp.dot(chooser, shares[step], preferred_element_type=jnp.float32)]
  transfers between devices with their start and end apart: 8 -> 21, of which waited for: 6 -> 8; matrix products, arithmetic and copies ran while one was open for 10% -> 24% of each run, Pallas kernels for 0% -> 0%
where the time goes in v3:
time: 246 us
  waiting for transfers between devices  110 us (45%)
  starting transfers between devices  49.9 us (20%)
  matrix products  38.5 us (16%)
  local copies, waits for them, and re-layouts  25 us (10%)
  between operations  13.7 us (6%)
  other arithmetic  9.03 us (4%)
    psum x1, waiting for transfers between devices, per_device(): logits = lax.psum(partial_logits, 'gate')  35.3 us
    ppermute x3, waiting for transfers between devices, per_device(): shares.append(lax.ppermute(samples, 'gate', peers(gate_count, step)))  34.4 us
    ppermute x14, starting transfers between devices, hopped(): piece = lax.ppermute(piece, 'expert', links)  32.7 us
    all_to_all x2, waiting for transfers between devices, per_device(): lax.all_to_all(outgoing, 'expert', split_axis=0, concat_axis=0, tiled=True)  20.1 us
    ppermute x14, waiting for transfers between devices, hopped(): piece = lax.ppermute(piece, 'expert', links)  19.8 us
    unnamed x50, local copies, waits for them, and re-layouts  19.5 us
    dot_general x4, matrix products, per_device(): jnp.dot(incoming[:, place].reshape(group_count * capacity, share), weight...  14.7 us
    all_to_all x2, starting transfers between devices, per_device(): lax.all_to_all(outgoing, 'expert', split_axis=0, concat_axis=0, tiled=True)  10.1 us
  transfers between devices with their start and end apart: 21, of which 8 were waited for; matrix products, arithmetic and copies ran while one was open for 24% of the time, Pallas kernels for 0%

profile of v3, /device:TPU:0, one launch (start us, length us, event | category | flops | bytes accessed | tf_op | source)
XLA Modules:
  0.0 245.8 jit_solution(6497913580321967888)
XLA Ops:
  6.5 3.0 %collective-permute-start.8 = (bf16[768,1024]{1,0:T(8,128)(2,1)}, bf16[768,1024]{1,0:T(8,128)(2,1)S(1)}, u32[]{:S(2)}, u32[]{:S(2)}) collective-permute-start(bf16[768,1024]{1,0:T(8,128)(2,1)} %param.6), channel_id=1, source_target_pairs={{0,2},{1,3},{2,0},{3,1},{4,6},{5,7},{6,4},{7,5},{8,10},{9,11},{10,... | collective-permute-start | bytes 4718600 | tf_op jit(solution)/shard_map/ppermute | solution.py:47
  9.6 0.8 slice_reduce_fusion.6
  11.1 0.9 select_reduce_fusion
  12.0 0.7 convert_add_fusion
  12.7 0.7 fusion.62
  13.5 1.7 fusion.5
  15.2 0.7 fusion.3
  15.9 2.5 %convolution_convert_fusion.1 = bf16[768,1024]{1,0:T(8,128)(2,1)} fusion(bf16[768,768]{1,0:T(8,128)(2,1)S(1)} %fusion.3, bf16[768,1024]{1,0:T(8,128)(2,1)S(1)} %copy-done.2), kind=kOutput, calls=%fused_computation.28 | convolution fusion | flops 1208745984 | bytes 4325376 | tf_op jit(solution)/shard_map/dot_general | solution.py:86
  18.5 6.4 %all-to-all-start = ((bf16[8,1,96,1024]{3,2,1,0:T(8,128)(2,1)}), bf16[8,1,96,1024]{3,2,1,0:T(8,128)(2,1)}, u32[]{:S(2)}, u32[]{:S(2)}) async-start(bf16[8,1,96,1024]{3,2,1,0:T(8,128)(2,1)} %bitcast.139), calls=%async_computation | async-start | bytes 3145728 | tf_op jit(solution)/shard_map/all_to_all | solution.py:92
  24.9 20.1 %collective-permute-done.8 = bf16[768,1024]{1,0:T(8,128)(2,1)S(1)} collective-permute-done((bf16[768,1024]{1,0:T(8,128)(2,1)}, bf16[768,1024]{1,0:T(8,128)(2,1)S(1)}, u32[]{:S(2)}, u32[]{:S(2)}) %collective-permute-start.8) | collective-permute-done | bytes 1572896 | tf_op jit(solution)/shard_map/ppermute | solution.py:47
  45.0 1.3 convolution_convert_fusion.12
  46.3 5.1 %collective-permute-start.9 = (bf16[96,1024]{1,0:T(8,128)(2,1)S(1)}, bf16[96,1024]{1,0:T(8,128)(2,1)S(1)}, u32[]{:S(2)}, u32[]{:S(2)}) collective-permute-start(bf16[96,1024]{1,0:T(8,128)(2,1)S(1)} %convolution_convert_fusion.12), channel_id=1, source_target_pairs={{0,28},{4,0},{8,4},{12,8},{16,12},{20,16},{24,20},{28,24},{1,29},{... | collective-permute-start | bytes 589832 | tf_op jit(solution)/shard_map/ppermute | solution.py:30
  51.4 1.3 convolution_convert_fusion.11
  53.7 1.1 constant_dynamic-update-slice_fusion.3
  56.4 3.0 %collective-permute-start.12 = (bf16[96,1024]{1,0:T(8,128)(2,1)S(1)}, bf16[96,1024]{1,0:T(8,128)(2,1)S(1)}, u32[]{:S(2)}, u32[]{:S(2)}) collective-permute-start(bf16[96,1024]{1,0:T(8,128)(2,1)S(1)} %convolution_convert_fusion.9), channel_id=1, source_target_pairs={{0,16},{4,20},{8,24},{12,28},{16,0},{20,4},{24,8},{28,12},{1,17},{... | collective-permute-start | bytes 589832 | tf_op jit(solution)/shard_map/ppermute | solution.py:30
  59.4 1.1 constant_dynamic-update-slice_fusion.1
  62.9 14.3 %collective-permute-done.16 = bf16[768,1024]{1,0:T(8,128)(2,1)} collective-permute-done((bf16[768,1024]{1,0:T(8,128)(2,1)}, bf16[768,1024]{1,0:T(8,128)(2,1)}, u32[]{:S(2)}, u32[]{:S(2)}) %collective-permute-start.16) | collective-permute-done | bytes 1572896 | tf_op jit(solution)/shard_map/ppermute | solution.py:47
  77.2 2.5 %collective-permute-start.13 = (bf16[96,1024]{1,0:T(8,128)(2,1)S(1)}, bf16[96,1024]{1,0:T(8,128)(2,1)S(1)}, u32[]{:S(2)}, u32[]{:S(2)}) collective-permute-start(bf16[96,1024]{1,0:T(8,128)(2,1)S(1)} %convolution_convert_fusion.8), channel_id=1, source_target_pairs={{0,12},{4,16},{8,20},{12,24},{16,28},{20,0},{24,4},{28,8},{1,13},{... | collective-permute-start | bytes 589832 | tf_op jit(solution)/shard_map/ppermute | solution.py:30
  79.7 4.0 %convolution_convert_fusion = bf16[768,1024]{1,0:T(8,128)(2,1)} fusion(bf16[768,768]{1,0:T(8,128)(2,1)S(1)} %copy-done.5, bf16[768,1024]{1,0:T(8,128)(2,1)} %collective-permute-done.16), kind=kOutput, calls=%fused_computation.27 | convolution fusion | flops 1208745984 | bytes 4325376 | tf_op jit(solution)/shard_map/dot_general | solution.py:86
  84.2 1.6 collective-permute-start.14
  85.8 0.7 bitcast_dynamic-update-slice_fusion.12
  86.5 1.5 collective-permute-start.15
  88.7 3.2 %collective-permute-start.1 = (bf16[96,1024]{1,0:T(8,128)(2,1)S(1)}, bf16[96,1024]{1,0:T(8,128)(2,1)S(1)}, u32[]{:S(2)}, u32[]{:S(2)}) collective-permute-start(bf16[96,1024]{1,0:T(8,128)(2,1)S(1)} %convolution_convert_fusion.20), channel_id=1, source_target_pairs={{0,28},{4,0},{8,4},{12,8},{16,12},{20,16},{24,20},{28,24},{1,29},{... | collective-permute-start | bytes 589832 | tf_op jit(solution)/shard_map/ppermute | solution.py:30
  92.6 4.4 %collective-permute-done.12 = bf16[96,1024]{1,0:T(8,128)(2,1)S(1)} collective-permute-done((bf16[96,1024]{1,0:T(8,128)(2,1)S(1)}, bf16[96,1024]{1,0:T(8,128)(2,1)S(1)}, u32[]{:S(2)}, u32[]{:S(2)}) %collective-permute-start.12) | collective-permute-done | bytes 196640 | tf_op jit(solution)/shard_map/ppermute | solution.py:30
  97.7 1.8 collective-permute-done.13
  100.2 9.7 %collective-permute-start.4 = (bf16[96,1024]{1,0:T(8,128)(2,1)S(1)}, bf16[96,1024]{1,0:T(8,128)(2,1)S(1)}, u32[]{:S(2)}, u32[]{:S(2)}) collective-permute-start(bf16[96,1024]{1,0:T(8,128)(2,1)S(1)} %convolution_convert_fusion.17), channel_id=1, source_target_pairs={{0,16},{4,20},{8,24},{12,28},{16,0},{20,4},{24,8},{28,12},{1,17},{... | collective-permute-start | bytes 589832 | tf_op jit(solution)/shard_map/ppermute | solution.py:30
  109.9 0.7 bitcast_dynamic-update-slice_fusion.2
  110.6 2.0 collective-permute-start.5
  112.6 0.7 bitcast_dynamic-update-slice_fusion
  114.0 3.4 %collective-permute-start.7 = (bf16[96,1024]{1,0:T(8,128)(2,1)S(1)}, bf16[96,1024]{1,0:T(8,128)(2,1)S(1)}, u32[]{:S(2)}, u32[]{:S(2)}) collective-permute-start(bf16[96,1024]{1,0:T(8,128)(2,1)S(1)} %convolution_convert_fusion.14), channel_id=1, source_target_pairs={{0,4},{4,8},{8,12},{12,16},{16,20},{20,24},{24,28},{28,0},{1,5},{5... | collective-permute-start | bytes 589832 | tf_op jit(solution)/shard_map/ppermute | solution.py:30
  117.4 0.7 bitcast_dynamic-update-slice_fusion.24
  118.1 0.7 bitcast_dynamic-update-slice_fusion.22
  118.8 10.7 %collective-permute-done.4 = bf16[96,1024]{1,0:T(8,128)(2,1)S(1)} collective-permute-done((bf16[96,1024]{1,0:T(8,128)(2,1)S(1)}, bf16[96,1024]{1,0:T(8,128)(2,1)S(1)}, u32[]{:S(2)}, u32[]{:S(2)}) %collective-permute-start.4) | collective-permute-done | bytes 196640 | tf_op jit(solution)/shard_map/ppermute | solution.py:30
  129.5 0.7 bitcast_dynamic-update-slice_fusion.20
  130.2 2.8 %collective-permute-done.5 = bf16[96,1024]{1,0:T(8,128)(2,1)S(1)} collective-permute-done((bf16[96,1024]{1,0:T(8,128)(2,1)S(1)}, bf16[96,1024]{1,0:T(8,128)(2,1)S(1)}, u32[]{:S(2)}, u32[]{:S(2)}) %collective-permute-start.5) | collective-permute-done | bytes 196640 | tf_op jit(solution)/shard_map/ppermute | solution.py:30
  133.0 0.7 bitcast_dynamic-update-slice_fusion.18
  133.7 0.7 constant_dynamic-update-slice_fusion.2
  134.5 0.7 bitcast_dynamic-update-slice_fusion.16
  135.8 0.7 constant_dynamic-update-slice_fusion
  136.5 0.7 bitcast_dynamic-update-slice_fusion.13
  137.9 0.7 bitcast_dynamic-update-slice_fusion.9
  138.6 0.7 bitcast_dynamic-update-slice_fusion.7
  139.3 0.7 bitcast_dynamic-update-slice_fusion.5
  140.0 0.7 bitcast_dynamic-update-slice_fusion.3
  142.1 0.7 bitcast_dynamic-update-slice_fusion.25
  142.8 3.8 %all-to-all-start.1 = ((bf16[8,1,96,1024]{3,2,1,0:T(8,128)(2,1)}), bf16[8,1,96,1024]{3,2,1,0:T(8,128)(2,1)S(1)}, u32[]{:S(2)}, u32[]{:S(2)}) async-start(bf16[8,1,96,1024]{3,2,1,0:T(8,128)(2,1)} %bitcast.26), calls=%async_computation.1 | async-start | bytes 3145728 | tf_op jit(solution)/shard_map/all_to_all | solution.py:92
  146.6 0.7 bitcast_dynamic-update-slice_fusion.23
  147.3 1.7 constant_dynamic-slice_fusion
  149.7 0.7 bitcast_dynamic-update-slice_fusion.19
  151.1 0.7 bitcast_dynamic-update-slice_fusion.15
  151.8 1.6 constant_dynamic-slice_fusion.1
  153.4 3.6 %fusion.11 = f32[768,1024]{1,0:T(8,128)S(1)} fusion(bf16[768,1024]{1,0:T(8,128)(2,1)S(1)} %bitcast.143, bf16[1,4096,1024]{2,1,0:T(8,128)(2,1)} %param.10, s32[]{:T(128)S(6)} %select_n.62), kind=kOutput, calls=%fused_computation.19 | convolution fusion | flops 1610612736 | bytes 6815748 | tf_op jit(solution)/shard_map/dot_general | solution.py:97
  156.9 3.2 %fusion.13 = f32[768,1024]{1,0:T(8,128)S(1)} fusion(bf16[768,1024]{1,0:T(8,128)(2,1)} %bitcast.3, bf16[1,4096,1024]{2,1,0:T(8,128)(2,1)S(1)} %bitcast.148, s32[]{:T(128)S(6)} %select_n.60), kind=kOutput, calls=%fused_computation.21 | convolution fusion | flops 1610612736 | bytes 6815748 | tf_op jit(solution)/shard_map/dot_general | solution.py:97
  160.2 3.5 %add_add_fusion = f32[768,1024]{1,0:T(8,128)} fusion(f32[768,1024]{1,0:T(8,128)S(1)} %fusion.13, f32[768,1024]{1,0:T(8,128)S(1)} %fusion.11, bf16[768,1024]{1,0:T(8,128)(2,1)S(1)} %bitcast.142, bf16[1,4096,1024]{2,1,0:T(8,128)(2,1)S(1)} %bitcast.148, s32[]{:T(128)S(6)} %select_n.63), kind=kOutput, calls=%fused_computation.4 | convolution fusion | flops 1612185600 | bytes 13107204 | tf_op jit(solution)/shard_map/dot_general | solution.py:97
  163.6 20.1 %all-to-all-done.1 = bf16[8,1,96,1024]{3,2,1,0:T(8,128)(2,1)S(1)} async-done(((bf16[8,1,96,1024]{3,2,1,0:T(8,128)(2,1)}), bf16[8,1,96,1024]{3,2,1,0:T(8,128)(2,1)S(1)}, u32[]{:S(2)}, u32[]{:S(2)}) %all-to-all-start.1) | async-done | bytes 1572896 | tf_op jit(solution)/shard_map/all_to_all | solution.py:92
  183.8 4.5 %maximum_convert_fusion = bf16[768,1024]{1,0:T(8,128)(2,1)S(1)} fusion(f32[768,1024]{1,0:T(8,128)} %add_add_fusion, bf16[768,1024]{1,0:T(8,128)(2,1)S(1)} %bitcast.141, bf16[1,4096,1024]{2,1,0:T(8,128)(2,1)} %param.10, s32[]{:T(128)S(6)} %select_n.64), kind=kOutput, calls=%fused_computation.3 | convolution fusion | flops 1612972032 | bytes 8388612 | tf_op jit(solution)/shard_map/dot_general | solution.py:97
  190.6 1.3 pad_maximum_fusion
  191.9 3.7 %all-to-all-start.2 = ((bf16[32,96,256]{2,1,0:T(8,128)(2,1)}), bf16[32,96,256]{2,1,0:T(8,128)(2,1)S(1)}, u32[]{:S(2)}, u32[]{:S(2)}) async-start(bf16[32,96,256]{2,1,0:T(8,128)(2,1)} %bitcast.37), calls=%async_computation.2 | async-start | bytes 3145728 | tf_op jit(solution)/shard_map/all_to_all | solution.py:117
  195.9 1.2 fusion.68
  197.2 35.3 %all-reduce.2.cloned.1.call-done = f32[32,768]{1,0:T(8,128)} async-done(((f32[32,768]{1,0:T(8,128)}), f32[32,768]{1,0:T(8,128)}) %all-reduce.2.cloned.1.call-update) | async-done | bytes 98320 | tf_op jit(solution)/shard_map/psum | solution.py:67
  232.5 0.9 reduce_max.9
  233.5 0.9 fusion.67
  234.5 3.4 %fusion = f32[1536,256]{1,0:T(8,128)S(1)} fusion(bf16[3072,256]{1,0:T(8,128)(2,1)S(1)} %bitcast.140, s32[1536]{0:T(1024)S(1)} %eq.150), kind=kOutput, calls=%fused_computation.1 | convolution fusion | flops 2420637696 | bytes 3151872 | tf_op jit(solution)/shard_map/dot_general | solution.py:131
  238.0 1.0 fusion.30
  (79 shorter events, 16.5 us)
Async XLA Ops:
  6.5 189.4 %copy-start = (bf16[1024,32]{0,1:T(8,128)(2,1)S(1)}, bf16[1024,32]{0,1:T(8,128)(2,1)}, u32[]{:S(2)}) copy-start(bf16[1024,32]{0,1:T(8,128)(2,1)} %param.7) | copy-start | bytes 196612
  6.5 38.4 %collective-permute-start.8 = (bf16[768,1024]{1,0:T(8,128)(2,1)}, bf16[768,1024]{1,0:T(8,128)(2,1)S(1)}, u32[]{:S(2)}, u32[]{:S(2)}) collective-permute-start(bf16[768,1024]{1,0:T(8,128)(2,1)} %param.6), channel_id=1, source_target_pairs={{0,2},{1,3},{2,0},{3,1},{4,6},{5,7},{6,4},{7,5},{8,10},{9,11},{10,... | collective-permute-start | bytes 4718600 | tf_op jit(solution)/shard_map/ppermute | solution.py:47
  9.5 46.9 %collective-permute-start = (bf16[768,1024]{1,0:T(8,128)(2,1)}, bf16[768,1024]{1,0:T(8,128)(2,1)S(1)}, u32[]{:S(2)}, u32[]{:S(2)}) collective-permute-start(bf16[768,1024]{1,0:T(8,128)(2,1)} %param.6), channel_id=1, source_target_pairs={{0,1},{1,0},{2,3},{3,2},{4,5},{5,4},{6,7},{7,6},{8,9},{9,8},{10,11... | collective-permute-start | bytes 4718600 | tf_op jit(solution)/shard_map/ppermute | solution.py:47
  9.5 67.7 %collective-permute-start.16 = (bf16[768,1024]{1,0:T(8,128)(2,1)}, bf16[768,1024]{1,0:T(8,128)(2,1)}, u32[]{:S(2)}, u32[]{:S(2)}) collective-permute-start(bf16[768,1024]{1,0:T(8,128)(2,1)} %param.6), channel_id=1, source_target_pairs={{0,3},{1,2},{2,1},{3,0},{4,7},{5,6},{6,5},{7,4},{8,11},{9,10},{10,... | collective-permute-start | bytes 4718600 | tf_op jit(solution)/shard_map/ppermute | solution.py:47
  11.1 4.8 %copy-start.2 = (bf16[768,1024]{1,0:T(8,128)(2,1)S(1)}, bf16[768,1024]{1,0:T(8,128)(2,1)}, u32[]{:S(2)}) copy-start(bf16[768,1024]{1,0:T(8,128)(2,1)} %param.6) | copy-start | bytes 4718596
  15.9 2.6 %copy-start.4 = (bf16[768,768]{1,0:T(8,128)(2,1)}, bf16[768,768]{1,0:T(8,128)(2,1)S(1)}, u32[]{:S(2)}) copy-start(bf16[768,768]{1,0:T(8,128)(2,1)S(1)} %fusion.3) | copy-start | bytes 3538948
  18.5 124.4 %all-to-all-start = ((bf16[8,1,96,1024]{3,2,1,0:T(8,128)(2,1)}), bf16[8,1,96,1024]{3,2,1,0:T(8,128)(2,1)}, u32[]{:S(2)}, u32[]{:S(2)}) async-start(bf16[8,1,96,1024]{3,2,1,0:T(8,128)(2,1)} %bitcast.139), calls=%async_computation | async-start | bytes 3145728 | tf_op jit(solution)/shard_map/all_to_all | solution.py:92
  24.8 28.4 %copy-start.1 = (bf16[768,768]{1,0:T(8,128)(2,1)S(1)}, bf16[768,768]{1,0:T(8,128)(2,1)}, u32[]{:S(2)}) copy-start(bf16[768,768]{1,0:T(8,128)(2,1)} %fusion.5) | copy-start | bytes 3538948
  46.3 37.9 %collective-permute-start.9 = (bf16[96,1024]{1,0:T(8,128)(2,1)S(1)}, bf16[96,1024]{1,0:T(8,128)(2,1)S(1)}, u32[]{:S(2)}, u32[]{:S(2)}) collective-permute-start(bf16[96,1024]{1,0:T(8,128)(2,1)S(1)} %convolution_convert_fusion.12), channel_id=1, source_target_pairs={{0,28},{4,0},{8,4},{12,8},{16,12},{20,16},{24,20},{28,24},{1,29},{... | collective-permute-start | bytes 589832 | tf_op jit(solution)/shard_map/ppermute | solution.py:30
  52.7 33.8 %collective-permute-start.10 = (bf16[96,1024]{1,0:T(8,128)(2,1)S(1)}, bf16[96,1024]{1,0:T(8,128)(2,1)S(1)}, u32[]{:S(2)}, u32[]{:S(2)}) collective-permute-start(bf16[96,1024]{1,0:T(8,128)(2,1)S(1)} %convolution_convert_fusion.11), channel_id=1, source_target_pairs={{0,24},{4,28},{8,0},{12,4},{16,8},{20,12},{24,16},{28,20},{1,25},{... | collective-permute-start | bytes 589832 | tf_op jit(solution)/shard_map/ppermute | solution.py:30
  53.6 35.1 %collective-permute-start.11 = (bf16[96,1024]{1,0:T(8,128)(2,1)S(1)}, bf16[96,1024]{1,0:T(8,128)(2,1)S(1)}, u32[]{:S(2)}, u32[]{:S(2)}) collective-permute-start(bf16[96,1024]{1,0:T(8,128)(2,1)S(1)} %convolution_convert_fusion.10), channel_id=1, source_target_pairs={{0,20},{4,24},{8,28},{12,0},{16,4},{20,8},{24,12},{28,16},{1,21},{... | collective-permute-start | bytes 589832 | tf_op jit(solution)/shard_map/ppermute | solution.py:30
  56.4 40.6 %collective-permute-start.12 = (bf16[96,1024]{1,0:T(8,128)(2,1)S(1)}, bf16[96,1024]{1,0:T(8,128)(2,1)S(1)}, u32[]{:S(2)}, u32[]{:S(2)}) collective-permute-start(bf16[96,1024]{1,0:T(8,128)(2,1)S(1)} %convolution_convert_fusion.9), channel_id=1, source_target_pairs={{0,16},{4,20},{8,24},{12,28},{16,0},{20,4},{24,8},{28,12},{1,17},{... | collective-permute-start | bytes 589832 | tf_op jit(solution)/shard_map/ppermute | solution.py:30
  62.1 17.6 %copy-start.5 = (bf16[768,768]{1,0:T(8,128)(2,1)S(1)}, bf16[768,768]{1,0:T(8,128)(2,1)}, u32[]{:S(2)}) copy-start(bf16[768,768]{1,0:T(8,128)(2,1)} %copy-done.4) | copy-start | bytes 3538948
  77.2 22.3 %collective-permute-start.13 = (bf16[96,1024]{1,0:T(8,128)(2,1)S(1)}, bf16[96,1024]{1,0:T(8,128)(2,1)S(1)}, u32[]{:S(2)}, u32[]{:S(2)}) collective-permute-start(bf16[96,1024]{1,0:T(8,128)(2,1)S(1)} %convolution_convert_fusion.8), channel_id=1, source_target_pairs={{0,12},{4,16},{8,20},{12,24},{16,28},{20,0},{24,4},{28,8},{1,13},{... | collective-permute-start | bytes 589832 | tf_op jit(solution)/shard_map/ppermute | solution.py:30
  84.2 16.0 %collective-permute-start.14 = (bf16[96,1024]{1,0:T(8,128)(2,1)S(1)}, bf16[96,1024]{1,0:T(8,128)(2,1)S(1)}, u32[]{:S(2)}, u32[]{:S(2)}) collective-permute-start(bf16[96,1024]{1,0:T(8,128)(2,1)S(1)} %convolution_convert_fusion.7), channel_id=1, source_target_pairs={{0,8},{4,12},{8,16},{12,20},{16,24},{20,28},{24,0},{28,4},{1,9},{5... | collective-permute-start | bytes 589832 | tf_op jit(solution)/shard_map/ppermute | solution.py:30
  86.5 24.1 %collective-permute-start.15 = (bf16[96,1024]{1,0:T(8,128)(2,1)S(1)}, bf16[96,1024]{1,0:T(8,128)(2,1)S(1)}, u32[]{:S(2)}, u32[]{:S(2)}) collective-permute-start(bf16[96,1024]{1,0:T(8,128)(2,1)S(1)} %convolution_convert_fusion.6), channel_id=1, source_target_pairs={{0,4},{4,8},{8,12},{12,16},{16,20},{20,24},{24,28},{28,0},{1,5},{5... | collective-permute-start | bytes 589832 | tf_op jit(solution)/shard_map/ppermute | solution.py:30
  88.7 24.6 %collective-permute-start.1 = (bf16[96,1024]{1,0:T(8,128)(2,1)S(1)}, bf16[96,1024]{1,0:T(8,128)(2,1)S(1)}, u32[]{:S(2)}, u32[]{:S(2)}) collective-permute-start(bf16[96,1024]{1,0:T(8,128)(2,1)S(1)} %convolution_convert_fusion.20), channel_id=1, source_target_pairs={{0,28},{4,0},{8,4},{12,8},{16,12},{20,16},{24,20},{28,24},{1,29},{... | collective-permute-start | bytes 589832 | tf_op jit(solution)/shard_map/ppermute | solution.py:30
  97.0 17.0 %collective-permute-start.2 = (bf16[96,1024]{1,0:T(8,128)(2,1)S(1)}, bf16[96,1024]{1,0:T(8,128)(2,1)S(1)}, u32[]{:S(2)}, u32[]{:S(2)}) collective-permute-start(bf16[96,1024]{1,0:T(8,128)(2,1)S(1)} %convolution_convert_fusion.19), channel_id=1, source_target_pairs={{0,24},{4,28},{8,0},{12,4},{16,8},{20,12},{24,16},{28,20},{1,25},{... | collective-permute-start | bytes 589832 | tf_op jit(solution)/shard_map/ppermute | solution.py:30
  99.5 18.6 %collective-permute-start.3 = (bf16[96,1024]{1,0:T(8,128)(2,1)S(1)}, bf16[96,1024]{1,0:T(8,128)(2,1)S(1)}, u32[]{:S(2)}, u32[]{:S(2)}) collective-permute-start(bf16[96,1024]{1,0:T(8,128)(2,1)S(1)} %convolution_convert_fusion.18), channel_id=1, source_target_pairs={{0,20},{4,24},{8,28},{12,0},{16,4},{20,8},{24,12},{28,16},{1,21},{... | collective-permute-start | bytes 589832 | tf_op jit(solution)/shard_map/ppermute | solution.py:30
  100.2 29.3 %collective-permute-start.4 = (bf16[96,1024]{1,0:T(8,128)(2,1)S(1)}, bf16[96,1024]{1,0:T(8,128)(2,1)S(1)}, u32[]{:S(2)}, u32[]{:S(2)}) collective-permute-start(bf16[96,1024]{1,0:T(8,128)(2,1)S(1)} %convolution_convert_fusion.17), channel_id=1, source_target_pairs={{0,16},{4,20},{8,24},{12,28},{16,0},{20,4},{24,8},{28,12},{1,17},{... | collective-permute-start | bytes 589832 | tf_op jit(solution)/shard_map/ppermute | solution.py:30
  110.6 22.4 %collective-permute-start.5 = (bf16[96,1024]{1,0:T(8,128)(2,1)S(1)}, bf16[96,1024]{1,0:T(8,128)(2,1)S(1)}, u32[]{:S(2)}, u32[]{:S(2)}) collective-permute-start(bf16[96,1024]{1,0:T(8,128)(2,1)S(1)} %convolution_convert_fusion.16), channel_id=1, source_target_pairs={{0,12},{4,16},{8,20},{12,24},{16,28},{20,0},{24,4},{28,8},{1,13},{... | collective-permute-start | bytes 589832 | tf_op jit(solution)/shard_map/ppermute | solution.py:30
  113.3 21.1 %collective-permute-start.6 = (bf16[96,1024]{1,0:T(8,128)(2,1)S(1)}, bf16[96,1024]{1,0:T(8,128)(2,1)S(1)}, u32[]{:S(2)}, u32[]{:S(2)}) collective-permute-start(bf16[96,1024]{1,0:T(8,128)(2,1)S(1)} %convolution_convert_fusion.15), channel_id=1, source_target_pairs={{0,8},{4,12},{8,16},{12,20},{16,24},{20,28},{24,0},{28,4},{1,9},{5... | collective-permute-start | bytes 589832 | tf_op jit(solution)/shard_map/ppermute | solution.py:30
  114.0 21.2 %collective-permute-start.7 = (bf16[96,1024]{1,0:T(8,128)(2,1)S(1)}, bf16[96,1024]{1,0:T(8,128)(2,1)S(1)}, u32[]{:S(2)}, u32[]{:S(2)}) collective-permute-start(bf16[96,1024]{1,0:T(8,128)(2,1)S(1)} %convolution_convert_fusion.14), channel_id=1, source_target_pairs={{0,4},{4,8},{8,12},{12,16},{16,20},{20,24},{24,28},{28,0},{1,5},{5... | collective-permute-start | bytes 589832 | tf_op jit(solution)/shard_map/ppermute | solution.py:30
  142.8 40.9 %all-to-all-start.1 = ((bf16[8,1,96,1024]{3,2,1,0:T(8,128)(2,1)}), bf16[8,1,96,1024]{3,2,1,0:T(8,128)(2,1)S(1)}, u32[]{:S(2)}, u32[]{:S(2)}) async-start(bf16[8,1,96,1024]{3,2,1,0:T(8,128)(2,1)} %bitcast.26), calls=%async_computation.1 | async-start | bytes 3145728 | tf_op jit(solution)/shard_map/all_to_all | solution.py:92
  147.3 9.6 %slice-start = ((s8[8388608]{0:T(1024)(128)(4,1)}), s8[4194304]{0:T(1024)(128)(4,1)S(1)}, s32[]{:S(2)}) async-start(s8[8388608]{0:T(1024)(128)(4,1)} %bitcast.147), calls=%async_computation.4 | async-start | bytes 8388608
  153.3 3.6 %slice-start.1 = ((s8[8388608]{0:T(1024)(128)(4,1)}), s8[4194304]{0:T(1024)(128)(4,1)S(1)}, s32[]{:S(2)}) async-start(s8[8388608]{0:T(1024)(128)(4,1)} %bitcast.147), calls=%async_computation.5 | async-start | bytes 8388608
  183.8 4.5 %copy-start.8 = (bf16[1,1024,1024]{2,1,0:T(8,128)(2,1)S(1)}, bf16[1,1024,1024]{2,1,0:T(8,128)(2,1)}, u32[]{:S(2)}) copy-start(bf16[1,1024,1024]{2,1,0:T(8,128)(2,1)} %param.11) | copy-start | bytes 6291460
  191.9 4.0 %copy-start.3 = (bf16[768,1024]{1,0:T(8,128)(2,1)S(1)}, bf16[768,1024]{1,0:T(8,128)(2,1)}, u32[]{:S(2)}) copy-start(bf16[768,1024]{1,0:T(8,128)(2,1)} %param.6) | copy-start | bytes 4718596
  191.9 5.3 %copy-start.7 = (s32[768]{0:T(1024)S(1)}, s32[768]{0:T(1024)}, u32[]{:S(2)}) copy-start(s32[768]{0:T(1024)} %param.9) | copy-start | bytes 9220
  191.9 42.5 %copy-start.6 = (s32[768,2]{0,1:T(2,128)S(1)}, s32[768,2]{0,1:T(2,128)}, u32[]{:S(2)}) copy-start(s32[768,2]{0,1:T(2,128)} %param.8) | copy-start | bytes 18436
  191.9 42.6 %all-to-all-start.2 = ((bf16[32,96,256]{2,1,0:T(8,128)(2,1)}), bf16[32,96,256]{2,1,0:T(8,128)(2,1)S(1)}, u32[]{:S(2)}, u32[]{:S(2)}) async-start(bf16[32,96,256]{2,1,0:T(8,128)(2,1)} %bitcast.37), calls=%async_computation.2 | async-start | bytes 3145728 | tf_op jit(solution)/shard_map/all_to_all | solution.py:117
  195.6 36.9 %all-reduce.2.cloned.1.call-start = ((), (), s32[]{:S(2)}) async-start(), calls=%async_computation.3 | async-start | bytes 196608 | tf_op jit(solution)/shard_map/psum | solution.py:67
Sparse Core Ops, SparseCore 0:
  198.8 33.7 all-reduce.1
